TPU v7x, 8 devices: a whole 2x2x1 slice. The times are simulated.
8 devices in a mesh: batch: 1 (over z), z: 2 (over y), y: 2 (over x), x: 2 (over core).
Axes of the slice: x: 2, y: 2, z: 1, core: 2. Of those that a mesh axis runs over, the one named last changes fastest.
Arguments:
- volume: bfloat16 [64, 128, 128, 128], P('batch', 'x', 'y', 'z')
- filter_taps: float32 [3, 3, 21], replicated
- mix_w: bfloat16 [3, 64, 64], replicated
- mix_bias: float32 [3, 64], replicated
Outputs:
- output: bfloat16 [64, 128, 128, 128], P('batch', 'x', 'y', 'z')
All inputs are finite; a program needn't handle non-finite values.
Results may differ from a plain program's by a relative error of at most 0.00616.
Values are sent between devices in bfloat16 or wider.
A program may use at most 1 GiB of HBM per device.

v0:
```python
import functools

import jax
import jax.numpy as jnp
from jax import lax
from jax.experimental import pallas as pl
from jax.experimental.pallas import tpu as pltpu
from jax.sharding import PartitionSpec as P


CI = 16
NT = (((1,), (1,)), ((), ()))
KB = 16
XQ = 4
YI = 4
YQ = 4
ZQ = 4
LJ = 16
LQ = 4
EJ = 16
EQ = 4
PAD = 1
LANES = 128
F32 = jnp.float32
BF16 = jnp.bfloat16


def toeplitz(taps, offset):
    half = (taps.shape[1] - 1) // 2
    hits = (offset + half)[None, ..., None] == jnp.arange(taps.shape[1])
    taps_b = taps.astype(BF16).astype(F32)
    return jnp.sum(jnp.where(hits, taps_b[:, None, None, :], 0.0), axis=-1).astype(BF16)


def band_x(taps, x_pos):
    n = jnp.arange(2 * CI)[:, None]
    q = jnp.arange(4 * CI)[None, :]
    sign = jnp.where(x_pos == 0, 1, -1)
    return toeplitz(taps, sign * CI * (q // CI - 1 - n // CI) + q % CI - n % CI)


FAR = 10**6


def band_y(taps, y_pos, jl_len):
    half = (taps.shape[1] - 1) // 2
    n = jnp.arange(jl_len)[:, None]
    m = jnp.arange(jl_len)
    r = jnp.arange(16)
    other = jnp.where(m < jl_len // 2, m + jl_len, m - jl_len)
    beyond = jnp.where(r < half, jnp.where(y_pos == 0, jl_len + r, r - half), FAR)
    return toeplitz(taps, jnp.concatenate([m, other, beyond])[None, :] - n)


def band_z(taps, z_pos, k_len):
    half = (taps.shape[1] - 1) // 2
    n = jnp.arange(k_len)[:, None]
    r = jnp.arange(16)
    beyond = jnp.where(r < half, jnp.where(z_pos == 0, k_len + r, r - half), FAR)
    return toeplitz(taps, jnp.concatenate([jnp.arange(k_len), beyond])[None, :] - n)


def lane_low(shape):
    return lax.broadcasted_iota(jnp.int32, shape, 1) < LANES // 2


def swap_halves(v):
    return pltpu.roll(v, LANES // 2, 1)


def x_kernel(n_in, half, meta, a_ref, *refs):
    vols, u_ref, sends, s_ref = refs[:n_in], refs[n_in], refs[n_in + 1 : -1], refs[-1]
    jl_len, ci = vols[0].shape[0], vols[0].shape[2]
    planes = len(sends) * ci
    row = planes + PAD
    y_pos = meta[1]
    first = jnp.where(y_pos == 0, jl_len - half, 0)
    group = 8
    mat = a_ref[0]

    def pair(kp, slot):
        for par in range(2):
            k = kp * 2 + par
            for g in range(0, jl_len, group):
                rhs = jnp.concatenate(
                    [jnp.concatenate([v[jl, k] for v in vols], axis=0) for jl in range(g, g + group)], axis=1
                )
                out = jnp.dot(mat, rhs, preferred_element_type=F32)
                for t in range(group):
                    s_ref[slot + par, pl.ds((g + t) * row, planes), :] = out[:, t * LANES : (t + 1) * LANES]

    def finish(kp, slot):
        for par in range(2):
            for i in range(planes):
                u_ref[i, kp * 2 + par] = s_ref[slot + par, pl.ds(i, jl_len, stride=row), :].astype(BF16)
        for r in range(half):
            for part, send_ref in enumerate(sends):
                rows = pl.ds((first + r) * row + part * ci, ci)
                even, odd = s_ref[slot, rows, :], s_ref[slot + 1, rows, :]
                low = lane_low(even.shape)
                up = jnp.where(low, swap_halves(even), odd)
                down = jnp.where(low, even, swap_halves(odd))
                send_ref[kp, r] = jnp.where(y_pos == 0, up, down).astype(BF16)

    def body(step, _):
        for q in range(XQ):
            pair(step * XQ + q, 2 * q)
            if q:
                finish(step * XQ + q - 1, 2 * (q - 1))
        finish(step * XQ + XQ - 1, 2 * (XQ - 1))
        return 0

    lax.fori_loop(0, vols[0].shape[1] // (2 * XQ), body, 0)


def x_pass(meta, mats, layer, vols, half):
    jl_len, k_len, ci, _ = vols[0].shape
    n_in, n_own = len(vols), mats.shape[1] // CI
    vol_spec = pl.BlockSpec((jl_len, KB, ci, LANES), lambda s, m: (0, s, 0, 0))
    send_spec = pl.BlockSpec((KB // 2, half, ci, LANES), lambda s, m: (s, 0, 0, 0))
    send_shape = jax.ShapeDtypeStruct((k_len // 2, half, ci, LANES), BF16)
    size = jl_len * k_len * ci * LANES
    return pl.pallas_call(
        functools.partial(x_kernel, n_in, half),
        grid_spec=pltpu.PrefetchScalarGridSpec(
            num_scalar_prefetch=1,
            grid=(k_len // KB,),
            in_specs=[pl.BlockSpec((1, *mats.shape[1:]), lambda s, m: (layer, 0, 0))] + [vol_spec] * n_in,
            out_specs=[pl.BlockSpec((n_own * ci, KB, jl_len, LANES), lambda s, m: (0, s, 0, 0))] + [send_spec] * n_own,
            scratch_shapes=[pltpu.VMEM((2 * XQ, jl_len * (n_own * ci + PAD), LANES), F32)],
        ),
        out_shape=[jax.ShapeDtypeStruct((n_own * ci, k_len, jl_len, LANES), BF16)] + [send_shape] * n_own,
        cost_estimate=pl.CostEstimate(flops=size * 512 * n_own, bytes_accessed=size * 2 * (n_in + n_own), transcendentals=0),
        name="x_pass",
    )(meta, mats, *vols)


def y_kernel(half, meta, a_ref, u_ref, nb_ref, o_ref, send_ref, nb_s, s_ref):
    y_pos, z_pos = meta[1], meta[2]
    k_len, jl_len = u_ref.shape[1], u_ref.shape[2]
    ci = nb_ref.shape[2]
    mat = a_ref[0]
    pitch = ci + PAD
    span = 16 * pitch
    row = jl_len + PAD

    @pl.when(pl.program_id(0) == 0)
    def _():
        def fill(kp, _):
            for r in range(16):
                rows = pl.ds(kp * span + r * pitch, ci)
                nb_s[rows, :] = nb_ref[kp, r].astype(F32) if r < half else jnp.zeros((ci, LANES), F32)
            return 0

        lax.fori_loop(0, k_len // 2, fill, 0)

    first = jnp.where(z_pos == 0, k_len - half, 0)

    def quad(here_i, slot, kq):
        i = pl.program_id(0) * YI + here_i
        parts = []
        for pr in range(2):
            kp = kq * 2 + pr
            nb = nb_s[pl.ds(kp * span + i, 16, stride=pitch), :]
            turned = swap_halves(nb)
            here = lane_low(nb.shape) == (y_pos != 0)
            for par in range(2):
                k = kp * 2 + par
                own = u_ref[here_i, k]
                other = swap_halves(own.astype(F32))
                top = lax.broadcasted_iota(jnp.int32, other.shape, 0) < jl_len // 2
                other = jnp.where(top == lane_low(other.shape), other, 0.0).astype(BF16)
                stay = (y_pos == 0) if par else (y_pos != 0)
                far = jnp.where(here, jnp.where(stay, nb, turned), 0.0).astype(BF16)
                parts.append(jnp.concatenate([own, other, far], axis=0))
        out = jnp.dot(mat, jnp.concatenate(parts, axis=1), preferred_element_type=F32)
        for t in range(4):
            rows = pl.ds((kq * 4 + t) * row, jl_len)
            s_ref[slot, rows, :] = out[:, t * LANES : (t + 1) * LANES]

    def finish(here_i, slot):
        for jl in range(jl_len):
            o_ref[here_i, jl] = s_ref[slot, pl.ds(jl, k_len, stride=row), :].astype(BF16)
        for r in range(half):
            for jb in range(jl_len // 8):
                rows = pl.ds((first + r) * row + jb * 8, 8)
                send_ref[here_i, jb, r] = s_ref[slot, rows, :].astype(BF16)

    def body(step, _):
        for q in range(YQ):
            for kq in range(k_len // 4):
                quad(step * YQ + q, q, kq)
            if q:
                finish(step * YQ + q - 1, q - 1)
        finish(step * YQ + YQ - 1, YQ - 1)
        return 0

    lax.fori_loop(0, YI // YQ, body, 0)


def y_pass(meta, mats, layer, u1, part, nb, half):

    ci, k_len, jl_len = nb.shape[2], u1.shape[1], u1.shape[2]
    size = jl_len * k_len * ci * LANES
    return pl.pallas_call(
        functools.partial(y_kernel, half),
        grid_spec=pltpu.PrefetchScalarGridSpec(
            num_scalar_prefetch=1,
            grid=(ci // YI,),
            in_specs=[
                pl.BlockSpec((1, *mats.shape[1:]), lambda s, m: (layer, 0, 0)),
                pl.BlockSpec((YI, k_len, jl_len, LANES), lambda s, m: (s + part * (ci // YI), 0, 0, 0)),
                pl.BlockSpec(nb.shape, lambda s, m: (0, 0, 0, 0)),
            ],
            out_specs=[
                pl.BlockSpec((YI, jl_len, k_len, LANES), lambda s, m: (s, 0, 0, 0)),
                pl.BlockSpec((YI, jl_len // 8, half, 8, LANES), lambda s, m: (s, 0, 0, 0, 0)),
            ],
            scratch_shapes=[
                pltpu.VMEM((k_len // 2 * 16 * (ci + PAD), LANES), F32),
                pltpu.VMEM((YQ, k_len * (jl_len + PAD), LANES), F32),
            ],
        ),
        out_shape=[
            jax.ShapeDtypeStruct((ci, jl_len, k_len, LANES), BF16),
            jax.ShapeDtypeStruct((ci, jl_len // 8, half, 8, LANES), BF16),
        ],
        cost_estimate=pl.CostEstimate(flops=size * 160 * 4, bytes_accessed=size * 5, transcendentals=0),
        name="y_pass",
    )(meta, mats, u1, nb)


class Mixer:
    def __init__(self, half, a_ref, w_ref, b_ref, u_ref, nb_ref, nb_s, u3_s):
        self.ci, self.jb, self.k_len = u_ref.shape[0], u_ref.shape[1], u_ref.shape[2]
        self.half, self.a_ref, self.w_ref, self.b_ref = half, a_ref, w_ref, b_ref
        self.u_ref, self.nb_ref, self.nb_s, self.u3_s = u_ref, nb_ref, nb_s, u3_s
        self.pitch = self.jb + PAD
        self.span = 16 * self.pitch

    def fill(self):
        def one(i, _):
            for r in range(16):
                rows = pl.ds(i * self.span + r * self.pitch, self.jb)
                far = self.nb_ref[i, 0, r].astype(F32) if r < self.half else jnp.zeros((self.jb, LANES), F32)
                self.nb_s[rows, :] = far
            return 0

        lax.fori_loop(0, self.ci, one, 0)

    def filt(self, jl, slot):
        for ip in range(self.ci // 2):
            parts = []
            for i in (2 * ip, 2 * ip + 1):
                far = self.nb_s[pl.ds(i * self.span + jl, 16, stride=self.pitch), :].astype(BF16)
                parts.append(jnp.concatenate([self.u_ref[i, jl], far], axis=0))
            u3 = jnp.dot(self.a_ref[0], jnp.concatenate(parts, axis=1), preferred_element_type=F32)
            self.u3_s[slot, pl.ds(ip * self.k_len, self.k_len), :] = u3.astype(BF16)

    def gelu(self, ip, slot):
        u3 = self.u3_s[slot, pl.ds(ip * self.k_len, self.k_len), :]
        m = jnp.dot(u3, self.w_ref[0], preferred_element_type=F32) + self.b_ref[0]
        return 0.5 * m * (1.0 + lax.erf(m * 0.7071067811865476))


def z_kernel(half, a_ref, w_ref, b_ref, u_ref, nb_ref, v_ref, o_ref, nb_s, u3_s, g_s):
    mixer = Mixer(half, a_ref, w_ref, b_ref, u_ref, nb_ref, nb_s, u3_s)
    ci, k_len = mixer.ci, mixer.k_len
    row = k_len + PAD
    mixer.fill()

    def mix(slot):
        for ip in range(ci // 2):
            g = mixer.gelu(ip, slot)
            for t in range(2):
                g_s[slot, pl.ds((2 * ip + t) * row, k_len), :] = g[:, t * LANES : (t + 1) * LANES]

    def finish(jl, slot):
        for k in range(k_len):
            g = g_s[slot, pl.ds(k, ci, stride=row), :]
            o_ref[jl, k] = (v_ref[jl, k].astype(F32) + g).astype(BF16)

    def body(step, _):
        for q in range(ZQ):
            mixer.filt(step * ZQ + q, q)
        for q in range(ZQ):
            mix(q)
            if q:
                finish(step * ZQ + q - 1, q - 1)
        finish(step * ZQ + ZQ - 1, ZQ - 1)
        return 0

    lax.fori_loop(0, mixer.jb // ZQ, body, 0)


def z_mix(mats, w4, bias, layer, u2, nb, vol, half):

    ci, jl_len, k_len, _ = u2.shape
    size = jl_len * k_len * ci * LANES
    vol_spec = pl.BlockSpec((8, k_len, ci, LANES), lambda s: (s, 0, 0, 0))
    return pl.pallas_call(
        functools.partial(z_kernel, half),
        grid=(jl_len // 8,),
        in_specs=[
            pl.BlockSpec((1, *mats.shape[1:]), lambda s: (layer, 0, 0)),
            pl.BlockSpec((1, *w4.shape[1:]), lambda s: (layer, 0, 0)),
            pl.BlockSpec((1, *bias.shape[1:]), lambda s: (layer, 0, 0)),
            pl.BlockSpec((ci, 8, k_len, LANES), lambda s: (0, s, 0, 0)),
            pl.BlockSpec((ci, 1, half, 8, LANES), lambda s: (0, s, 0, 0, 0)),
            vol_spec,
        ],
        out_specs=vol_spec,
        scratch_shapes=[
            pltpu.VMEM((ci * 16 * (8 + PAD), LANES), F32),
            pltpu.VMEM((ZQ, ci // 2 * k_len, 2 * LANES), BF16),
            pltpu.VMEM((ZQ, ci * (k_len + PAD), LANES), F32),
        ],
        out_shape=jax.ShapeDtypeStruct(vol.shape, BF16),
        cost_estimate=pl.CostEstimate(flops=size * 160 * 6, bytes_accessed=size * 7, transcendentals=size),
        name="z_mix",
    )(mats, w4, bias, u2, nb, vol)


def enter_kernel(meta, eye_ref, lo_ref, hi_ref, o_ref, s_ref, t_ref):
    chans, ci, jb, k_len = lo_ref.shape
    eye = eye_ref[...]
    pitch, row = jb + PAD, k_len + PAD

    def spread(c, _):
        for h, ref in enumerate((lo_ref, hi_ref)):
            for ip in range(ci // 2):
                rows = pl.ds(((ip * 2 + h) * chans + c) * pitch, jb)
                s_ref[rows, :] = jnp.concatenate([ref[c, 2 * ip].astype(F32), ref[c, 2 * ip + 1].astype(F32)], axis=1)
        return 0

    lax.fori_loop(0, chans, spread, 0, unroll=16)

    def turn(jl, slot):
        for ip in range(0, ci // 2, 2):
            parts = [
                s_ref[pl.ds((ip + u) * 2 * chans * pitch + jl, 2 * chans, stride=pitch), :].astype(BF16) for u in range(2)
            ]
            out = lax.dot_general(eye, jnp.concatenate(parts, axis=0), NT, preferred_element_type=F32)
            for u in range(2):
                for t in range(2):
                    done = out[t * k_len : (t + 1) * k_len, u * LANES : (u + 1) * LANES]
                    t_ref[slot, pl.ds((2 * (ip + u) + t) * row, k_len), :] = done

    def finish(jl, slot):
        for k in range(k_len):
            o_ref[jl, k] = t_ref[slot, pl.ds(k, ci, stride=row), :].astype(BF16)

    def body(step, _):
        for q in range(EQ):
            turn(EQ * step + q, q)
            if q:
                finish(EQ * step + q - 1, q - 1)
        finish(EQ * step + EQ - 1, EQ - 1)
        return 0

    lax.fori_loop(0, jb // EQ, body, 0)


def enter(meta, volume, p, n_chunks):
    chans, _, j_len, k_len = volume.shape
    jl_len, jb = j_len // 2, EJ

    def spot(h):
        return lambda s, m: (0, jnp.where(m[0] == 0, p, n_chunks - 1 - p), s + h * (jl_len // jb), 0)

    blocks = [pl.BlockSpec((chans, CI, jb, k_len), spot(h)) for h in range(2)]
    size = chans * CI * j_len * k_len
    return pl.pallas_call(
        enter_kernel,
        grid_spec=pltpu.PrefetchScalarGridSpec(
            num_scalar_prefetch=1,
            grid=(jl_len // jb,),
            in_specs=[pl.BlockSpec((2 * k_len, 2 * k_len), lambda s, m: (0, 0))] + blocks,
            out_specs=pl.BlockSpec((jb, k_len, CI, 2 * chans), lambda s, m: (s, 0, 0, 0)),
            scratch_shapes=[
                pltpu.VMEM((CI * chans * (jb + PAD), 2 * k_len), F32),
                pltpu.VMEM((EQ, CI * (k_len + PAD), 2 * chans), F32),
            ],
        ),
        out_shape=jax.ShapeDtypeStruct((jl_len, k_len, CI, 2 * chans), BF16),
        cost_estimate=pl.CostEstimate(flops=size * 512, bytes_accessed=size * 6, transcendentals=0),
        name="enter",
    )(meta, jnp.eye(2 * k_len, dtype=BF16), volume, volume)


def leave_kernel(meta, eye_ref, v_ref, *refs):
    o_ref, t_ref, s_ref = refs[-3:]
    jb, k_len, ci, lanes = v_ref.shape
    chans = lanes // 2
    h = pl.program_id(1)
    pitch, row = jb + PAD, ci + PAD
    eye = eye_ref[...]

    @pl.when(h == 0)
    def _():
        def spread(jl, slot):
            for k in range(k_len):
                t_ref[slot, pl.ds(k * row, ci), :] = v_ref[jl, k].astype(F32)

        def turn(jl, slot):
            for ip in range(0, ci // 2, 2):
                parts = [t_ref[slot, pl.ds(2 * ip + t, k_len, stride=row), :].astype(BF16) for t in range(4)]
                out = lax.dot_general(eye, jnp.concatenate(parts, axis=0), NT, preferred_element_type=F32)
                for u in range(2):
                    rows = pl.ds((ip + u) * lanes * pitch + jl, lanes, stride=pitch)
                    s_ref[rows, :] = out[:, u * LANES : (u + 1) * LANES]

        def body(step, _):
            for q in range(LQ):
                spread(LQ * step + q, q)
                if q:
                    turn(LQ * step + q - 1, q - 1)
            turn(LQ * step + LQ - 1, LQ - 1)
            return 0

        lax.fori_loop(0, jb // LQ, body, 0)

    def pack(c, _):
        for ip in range(ci // 2):
            both = s_ref[pl.ds((ip * lanes + h * chans + c) * pitch, jb), :]
            o_ref[c, 2 * ip] = both[:, :k_len].astype(BF16)
            o_ref[c, 2 * ip + 1] = swap_halves(both)[:, :k_len].astype(BF16)
        return 0

    lax.fori_loop(0, chans, pack, 0, unroll=16)


def leave(meta, vol, out, p, n_chunks):
    jl_len, k_len, ci, lanes = vol.shape
    chans, jb = lanes // 2, LJ
    j_len = 2 * jl_len

    def spot(s, h, m):
        return (0, jnp.where(m[0] == 0, p, n_chunks - 1 - p), s + h * (jl_len // jb), 0)

    size = chans * CI * j_len * k_len
    more = [] if out is None else [out]
    return pl.pallas_call(
        leave_kernel,
        grid_spec=pltpu.PrefetchScalarGridSpec(
            num_scalar_prefetch=1,
            grid=(jl_len // jb, 2),
            in_specs=[
                pl.BlockSpec((lanes, lanes), lambda s, h, m: (0, 0)),
                pl.BlockSpec((jb, k_len, ci, lanes), lambda s, h, m: (s, 0, 0, 0)),
            ]
            + [pl.BlockSpec(memory_space=pl.ANY) for _ in more],
            out_specs=pl.BlockSpec((chans, CI, jb, k_len), spot),
            scratch_shapes=[
                pltpu.VMEM((LQ, k_len * (ci + PAD), lanes), F32),
                pltpu.VMEM((CI // 2 * lanes * (jb + PAD), 2 * k_len), F32),
            ],
        ),
        out_shape=jax.ShapeDtypeStruct((chans, n_chunks * CI, j_len, k_len), BF16),
        input_output_aliases={3: 0} if more else {},
        cost_estimate=pl.CostEstimate(flops=size * 512, bytes_accessed=size * 6, transcendentals=0),
        name="leave",
    )(meta, jnp.eye(lanes, dtype=BF16), vol, *more)


SWAP = [(0, 1), (1, 0)]
ORDER = (
    "e3", "e2", "e1", "x031", "e0", "x021", "y03", "x002", "y02", "z03",
    "y00", "z02", "y01", "x131", "z00", "z01", "x101", "y13", "x112", "y10",
    "z13", "y11", "z10", "y12", "z11", "x201", "z12", "x231", "y20", "x212",
    "y23", "z20", "l0", "y21", "y22", "z23", "l3", "z21", "z22", "l2",
    "l1",
)


def solution(mesh):
    def local_layers(volume, filter_taps, mix_w, mix_bias):
        _, i_len, j_len, k_len = volume.shape
        layers = filter_taps.shape[0]
        half = (filter_taps.shape[2] - 1) // 2
        jl_len, n_chunks = j_len // 2, i_len // CI
        x_pos, y_pos, z_pos = (lax.axis_index(a) for a in ("x", "y", "z"))
        meta = jnp.stack([x_pos, y_pos, z_pos]).astype(jnp.int32)
        mats_x = band_x(filter_taps[:, 0], x_pos)
        mats_y = band_y(filter_taps[:, 1], y_pos, jl_len)
        mats_z = band_z(filter_taps[:, 2], z_pos, k_len)
        w4 = jax.vmap(lambda w: jnp.kron(jnp.eye(4, dtype=BF16), w))(mix_w)
        bias = jnp.tile(mix_bias, (1, 4))[:, None, :]

        vols, u2, far_y, far_z, beyond = {}, {}, {}, {}, {}
        out = None

        def settle(layer, p, vol):
            vols[layer, p] = vol
            if p == n_chunks - 1 and layer < layers:
                beyond[layer] = lax.ppermute(vol, "x", SWAP)

        for op in ORDER:
            kind, p = op[0], int(op[1] if op[0] in "el" else op[2])
            layer = int(op[1])
            if kind == "e":
                settle(0, p, enter(meta, volume, p, n_chunks))
            elif kind == "x":
                n_own = int(op[3])
                own = [vols[layer, q] for q in range(max(p - 1, 0), p + n_own)]
                after = vols[layer, p + n_own] if p + n_own < n_chunks else beyond[layer]
                first = 0 if p else CI
                mats = mats_x[:, : n_own * CI, first : (n_own + 2) * CI]
                u1, *send = x_pass(meta, mats, layer, own + [after], half)
                for t in range(n_own):
                    far_y[p + t] = (u1, t, lax.ppermute(send[t], "y", SWAP))
            elif kind == "y":
                u2[p], send = y_pass(meta, mats_y, layer, *far_y[p], half)
                far_z[p] = lax.ppermute(send, "z", SWAP)
            elif kind == "z":
                settle(layer + 1, p, z_mix(mats_z, w4, bias, layer, u2[p], far_z[p], vols[layer, p], half))
            else:
                out = leave(meta, vols[layers, p], out, p, n_chunks)
        return out

    vol_spec = P("batch", "x", "y", "z")
    return jax.shard_map(local_layers, mesh=mesh, in_specs=(vol_spec, P(), P(), P()), out_specs=vol_spec, check_vma=False)
```

profile of v0, /device:TPU:0, one launch (start us, length us, event | category | flops | bytes accessed | tf_op | source)
XLA Modules:
  0.0 888.0 jit_solution(15708660878663472193)
XLA Ops:
  29.8 15.0 %x_pass.12 = (bf16[16,64,32,128]{3,2,1,0:T(8,128)(2,1)}, bf16[32,10,16,128]{3,2,1,0:T(8,128)(2,1)}) custom-call(s32[3]{0:T(128)} %pad_add_fusion.meta, bf16[3,16,48]{2,1,0:T(8,128)(2,1)} %slice.36.a_ref, bf16[32,64,16,128]{3,2,1,0:T(8,128)(2,1)} %enter.6.refs_2_.refs_1_.v_ref.refs_0_, bf16[32,64,16,128]{3,2,1,0:T(8,128)(2,1)} %enter.7.refs_2_.refs_1_.v_ref, ...), custom_call_target="tpu_custom_call" | custom-call | flops 2147483648 | bytes 33554432 | tf_op jit(solution)/shard_map/x_pass/pallas_call | solution.py:123
  48.2 28.7 %collective-permute-done.9.nb_ref = bf16[32,10,16,128]{3,2,1,0:T(8,128)(2,1)S(1)} collective-permute-done((bf16[32,10,16,128]{3,2,1,0:T(8,128)(2,1)}, bf16[32,10,16,128]{3,2,1,0:T(8,128)(2,1)S(1)}, u32[]{:S(2)}, u32[]{:S(2)}) %collective-permute-start.9) | collective-permute-done | bytes 1310752 | tf_op jit(solution)/shard_map/ppermute | solution.py:511
  94.9 25.2 %collective-permute-done.10.nb_ref = bf16[16,4,10,8,128]{4,3,2,1,0:T(8,128)(2,1)S(1)} collective-permute-done((bf16[16,4,10,8,128]{4,3,2,1,0:T(8,128)(2,1)}, bf16[16,4,10,8,128]{4,3,2,1,0:T(8,128)(2,1)S(1)}, u32[]{:S(2)}, u32[]{:S(2)}) %collective-permute-start.10) | collective-permute-done | bytes 1310752 | tf_op jit(solution)/shard_map/ppermute | solution.py:514
  121.2 15.6 %z_mix.16.refs_3_.refs_1_.v_ref = bf16[32,64,16,128]{3,2,1,0:T(8,128)(2,1)} custom-call(bf16[3,64,80]{2,1,0:T(8,128)(2,1)} %select_reduce_fusion.a_ref, bf16[3,256,256]{2,1,0:T(8,128)(2,1)} %broadcast_multiply_fusion.w_ref, f32[3,1,256]{2,1,0:T(1,128)} %tile.9.b_ref, bf16[16,32,64,128]{3,2,1,0:T(8,128)(2,1)} %get-tuple-element.67.u_ref, ...), custom_call_target="tpu_custom_call" | custom-call | flops 4026531840 | bytes 29360128 | tf_op jit(solution)/shard_map/z_mix/pallas_call | solution.py:301
  150.1 15.1 %x_pass.11 = (bf16[16,64,32,128]{3,2,1,0:T(8,128)(2,1)}, bf16[32,10,16,128]{3,2,1,0:T(8,128)(2,1)}) custom-call(s32[3]{0:T(128)} %pad_add_fusion.meta, bf16[3,16,48]{2,1,0:T(8,128)(2,1)} %slice.36.a_ref, bf16[32,64,16,128]{3,2,1,0:T(8,128)(2,1)} %enter.5.refs_1_.v_ref.refs_0_, bf16[32,64,16,128]{3,2,1,0:T(8,128)(2,1)} %enter.6.refs_2_.refs_1_.v_ref.refs_0_, ...), custom_call_target="tpu_custom_call" | custom-call | flops 2147483648 | bytes 33554432 | tf_op jit(solution)/shard_map/x_pass/pallas_call | solution.py:123
  166.6 30.0 %collective-permute-done.6.nb_ref = bf16[32,10,16,128]{3,2,1,0:T(8,128)(2,1)S(1)} collective-permute-done((bf16[32,10,16,128]{3,2,1,0:T(8,128)(2,1)}, bf16[32,10,16,128]{3,2,1,0:T(8,128)(2,1)S(1)}, u32[]{:S(2)}, u32[]{:S(2)}) %collective-permute-start.6) | collective-permute-done | bytes 1310752 | tf_op jit(solution)/shard_map/ppermute | solution.py:511
  210.5 29.0 %collective-permute-done.7.nb_ref = bf16[16,4,10,8,128]{4,3,2,1,0:T(8,128)(2,1)S(1)} collective-permute-done((bf16[16,4,10,8,128]{4,3,2,1,0:T(8,128)(2,1)}, bf16[16,4,10,8,128]{4,3,2,1,0:T(8,128)(2,1)S(1)}, u32[]{:S(2)}, u32[]{:S(2)}) %collective-permute-start.7) | collective-permute-done | bytes 1310752 | tf_op jit(solution)/shard_map/ppermute | solution.py:514
  240.6 15.6 %z_mix.15.refs_2_.v_ref.refs_0_ = bf16[32,64,16,128]{3,2,1,0:T(8,128)(2,1)} custom-call(bf16[3,64,80]{2,1,0:T(8,128)(2,1)} %select_reduce_fusion.a_ref, bf16[3,256,256]{2,1,0:T(8,128)(2,1)} %broadcast_multiply_fusion.w_ref, f32[3,1,256]{2,1,0:T(1,128)} %tile.9.b_ref, bf16[16,32,64,128]{3,2,1,0:T(8,128)(2,1)} %get-tuple-element.63.u_ref, ...), custom_call_target="tpu_custom_call" | custom-call | flops 4026531840 | bytes 29360128 | tf_op jit(solution)/shard_map/z_mix/pallas_call | solution.py:301
  256.2 15.1 %x_pass.14 = (bf16[16,64,32,128]{3,2,1,0:T(8,128)(2,1)}, bf16[32,10,16,128]{3,2,1,0:T(8,128)(2,1)}) custom-call(s32[3]{0:T(128)} %pad_add_fusion.meta, bf16[3,16,48]{2,1,0:T(8,128)(2,1)} %slice.36.a_ref, bf16[32,64,16,128]{3,2,1,0:T(8,128)(2,1)} %z_mix.15.refs_2_.v_ref.refs_0_, bf16[32,64,16,128]{3,2,1,0:T(8,128)(2,1)} %z_mix.16.refs_3_.refs_1_.v_ref, ...), custom_call_target="tpu_custom_call" | custom-call | flops 2147483648 | bytes 33554432 | tf_op jit(solution)/shard_map/x_pass/pallas_call | solution.py:123
  272.7 28.3 %collective-permute-done.16.nb_ref = bf16[32,10,16,128]{3,2,1,0:T(8,128)(2,1)S(1)} collective-permute-done((bf16[32,10,16,128]{3,2,1,0:T(8,128)(2,1)}, bf16[32,10,16,128]{3,2,1,0:T(8,128)(2,1)S(1)}, u32[]{:S(2)}, u32[]{:S(2)}) %collective-permute-start.16) | collective-permute-done | bytes 1310752 | tf_op jit(solution)/shard_map/ppermute | solution.py:511
  328.9 21.0 %x_pass.9 = (bf16[32,64,32,128]{3,2,1,0:T(8,128)(2,1)}, bf16[32,10,16,128]{3,2,1,0:T(8,128)(2,1)}, bf16[32,10,16,128]{3,2,1,0:T(8,128)(2,1)}) custom-call(s32[3]{0:T(128)} %pad_add_fusion.meta, bf16[3,32,48]{2,1,0:T(8,128)(2,1)} %slice.35.a_ref, bf16[32,64,16,128]{3,2,1,0:T(8,128)(2,1)} %enter.4.refs_0_.v_ref, ...), custom_call_target="tpu_custom_call" | custom-call | flops 4294967296 | bytes 41943040 | tf_op jit(solution)/shard_map/x_pass/pallas_call | solution.py:123
  351.9 15.6 %z_mix.19.refs_3_.refs_1_.v_ref = bf16[32,64,16,128]{3,2,1,0:T(8,128)(2,1)} custom-call(bf16[3,64,80]{2,1,0:T(8,128)(2,1)} %select_reduce_fusion.a_ref, bf16[3,256,256]{2,1,0:T(8,128)(2,1)} %broadcast_multiply_fusion.w_ref, f32[3,1,256]{2,1,0:T(1,128)} %tile.9.b_ref, bf16[16,32,64,128]{3,2,1,0:T(8,128)(2,1)} %get-tuple-element.78.u_ref, ...), custom_call_target="tpu_custom_call" | custom-call | flops 4026531840 | bytes 29360128 | tf_op jit(solution)/shard_map/z_mix/pallas_call | solution.py:301
  367.6 14.2 %collective-permute-done.2.nb_ref = bf16[32,10,16,128]{3,2,1,0:T(8,128)(2,1)S(1)} collective-permute-done((bf16[32,10,16,128]{3,2,1,0:T(8,128)(2,1)}, bf16[32,10,16,128]{3,2,1,0:T(8,128)(2,1)S(1)}, u32[]{:S(2)}, u32[]{:S(2)}) %collective-permute-start.2) | collective-permute-done | bytes 1310752 | tf_op jit(solution)/shard_map/ppermute | solution.py:511
  421.2 15.6 %z_mix.13.refs_1_.v_ref = bf16[32,64,16,128]{3,2,1,0:T(8,128)(2,1)} custom-call(bf16[3,64,80]{2,1,0:T(8,128)(2,1)} %select_reduce_fusion.a_ref, bf16[3,256,256]{2,1,0:T(8,128)(2,1)} %broadcast_multiply_fusion.w_ref, f32[3,1,256]{2,1,0:T(1,128)} %tile.9.b_ref, bf16[16,32,64,128]{3,2,1,0:T(8,128)(2,1)} %get-tuple-element.55.u_ref, ...), custom_call_target="tpu_custom_call" | custom-call | flops 4026531840 | bytes 29360128 | tf_op jit(solution)/shard_map/z_mix/pallas_call | solution.py:301
  447.7 15.6 %z_mix.12.refs_0_.v_ref = bf16[32,64,16,128]{3,2,1,0:T(8,128)(2,1)} custom-call(bf16[3,64,80]{2,1,0:T(8,128)(2,1)} %select_reduce_fusion.a_ref, bf16[3,256,256]{2,1,0:T(8,128)(2,1)} %broadcast_multiply_fusion.w_ref, f32[3,1,256]{2,1,0:T(1,128)} %tile.9.b_ref, bf16[16,32,64,128]{3,2,1,0:T(8,128)(2,1)} %get-tuple-element.52.u_ref, ...), custom_call_target="tpu_custom_call" | custom-call | flops 4026531840 | bytes 29360128 | tf_op jit(solution)/shard_map/z_mix/pallas_call | solution.py:301
  463.3 13.4 %x_pass.10 = (bf16[16,64,32,128]{3,2,1,0:T(8,128)(2,1)}, bf16[32,10,16,128]{3,2,1,0:T(8,128)(2,1)}) custom-call(s32[3]{0:T(128)} %pad_add_fusion.meta, bf16[3,16,32]{2,1,0:T(8,128)(2,1)} %slice.34.a_ref, bf16[32,64,16,128]{3,2,1,0:T(8,128)(2,1)} %z_mix.12.refs_0_.v_ref, bf16[32,64,16,128]{3,2,1,0:T(8,128)(2,1)} %z_mix.13.refs_1_.v_ref), custom_call_target="tpu_custom_call" | custom-call | flops 2147483648 | bytes 25165824 | tf_op jit(solution)/shard_map/x_pass/pallas_call | solution.py:123
  477.9 23.4 %x_pass.13 = (bf16[32,64,32,128]{3,2,1,0:T(8,128)(2,1)}, bf16[32,10,16,128]{3,2,1,0:T(8,128)(2,1)}, bf16[32,10,16,128]{3,2,1,0:T(8,128)(2,1)}) custom-call(s32[3]{0:T(128)} %pad_add_fusion.meta, bf16[3,32,64]{2,1,0:T(8,128)(2,1)} %copy-done.12, bf16[32,64,16,128]{3,2,1,0:T(8,128)(2,1)} %z_mix.12.refs_0_.v_ref, ...), custom_call_target="tpu_custom_call" | custom-call | flops 4294967296 | bytes 50331648 | tf_op jit(solution)/shard_map/x_pass/pallas_call | solution.py:123
  520.1 15.4 %collective-permute-done.11.nb_ref = bf16[32,10,16,128]{3,2,1,0:T(8,128)(2,1)} collective-permute-done((bf16[32,10,16,128]{3,2,1,0:T(8,128)(2,1)}, bf16[32,10,16,128]{3,2,1,0:T(8,128)(2,1)}, u32[]{:S(2)}, u32[]{:S(2)}) %collective-permute-start.11) | collective-permute-done | bytes 1310752 | tf_op jit(solution)/shard_map/ppermute | solution.py:511
  573.7 15.6 %z_mix.14.refs_0_.v_ref = bf16[32,64,16,128]{3,2,1,0:T(8,128)(2,1)} custom-call(bf16[3,64,80]{2,1,0:T(8,128)(2,1)} %select_reduce_fusion.a_ref, bf16[3,256,256]{2,1,0:T(8,128)(2,1)} %broadcast_multiply_fusion.w_ref, f32[3,1,256]{2,1,0:T(1,128)} %tile.9.b_ref, bf16[16,32,64,128]{3,2,1,0:T(8,128)(2,1)} %get-tuple-element.59.u_ref, ...), custom_call_target="tpu_custom_call" | custom-call | flops 4026531840 | bytes 29360128 | tf_op jit(solution)/shard_map/z_mix/pallas_call | solution.py:301
  589.3 15.6 %z_mix.17.refs_1_.v_ref = bf16[32,64,16,128]{3,2,1,0:T(8,128)(2,1)} custom-call(bf16[3,64,80]{2,1,0:T(8,128)(2,1)} %select_reduce_fusion.a_ref, bf16[3,256,256]{2,1,0:T(8,128)(2,1)} %broadcast_multiply_fusion.w_ref, f32[3,1,256]{2,1,0:T(1,128)} %tile.9.b_ref, bf16[16,32,64,128]{3,2,1,0:T(8,128)(2,1)} %get-tuple-element.71.u_ref, ...), custom_call_target="tpu_custom_call" | custom-call | flops 4026531840 | bytes 29360128 | tf_op jit(solution)/shard_map/z_mix/pallas_call | solution.py:301
  620.6 15.6 %z_mix.18.refs_2_.v_ref.refs_0_ = bf16[32,64,16,128]{3,2,1,0:T(8,128)(2,1)} custom-call(bf16[3,64,80]{2,1,0:T(8,128)(2,1)} %select_reduce_fusion.a_ref, bf16[3,256,256]{2,1,0:T(8,128)(2,1)} %broadcast_multiply_fusion.w_ref, f32[3,1,256]{2,1,0:T(1,128)} %tile.9.b_ref, bf16[16,32,64,128]{3,2,1,0:T(8,128)(2,1)} %get-tuple-element.74.u_ref, ...), custom_call_target="tpu_custom_call" | custom-call | flops 4026531840 | bytes 29360128 | tf_op jit(solution)/shard_map/z_mix/pallas_call | solution.py:301
  636.2 23.0 %x_pass.15 = (bf16[32,64,32,128]{3,2,1,0:T(8,128)(2,1)}, bf16[32,10,16,128]{3,2,1,0:T(8,128)(2,1)}, bf16[32,10,16,128]{3,2,1,0:T(8,128)(2,1)}) custom-call(s32[3]{0:T(128)} %pad_add_fusion.meta, bf16[3,32,64]{2,1,0:T(8,128)(2,1)} %copy-done.12, bf16[32,64,16,128]{3,2,1,0:T(8,128)(2,1)} %z_mix.14.refs_0_.v_ref, ...), custom_call_target="tpu_custom_call" | custom-call | flops 4294967296 | bytes 50331648 | tf_op jit(solution)/shard_map/x_pass/pallas_call | solution.py:123
  661.2 15.0 %x_pass.16 = (bf16[16,64,32,128]{3,2,1,0:T(8,128)(2,1)}, bf16[32,10,16,128]{3,2,1,0:T(8,128)(2,1)}) custom-call(s32[3]{0:T(128)} %pad_add_fusion.meta, bf16[3,16,48]{2,1,0:T(8,128)(2,1)} %slice.36.a_ref, bf16[32,64,16,128]{3,2,1,0:T(8,128)(2,1)} %z_mix.18.refs_2_.v_ref.refs_0_, bf16[32,64,16,128]{3,2,1,0:T(8,128)(2,1)} %z_mix.19.refs_3_.refs_1_.v_ref, ...), custom_call_target="tpu_custom_call" | custom-call | flops 2147483648 | bytes 33554432 | tf_op jit(solution)/shard_map/x_pass/pallas_call | solution.py:123
  703.8 15.3 %collective-permute-done.18.nb_ref = bf16[32,10,16,128]{3,2,1,0:T(8,128)(2,1)S(1)} collective-permute-done((bf16[32,10,16,128]{3,2,1,0:T(8,128)(2,1)}, bf16[32,10,16,128]{3,2,1,0:T(8,128)(2,1)S(1)}, u32[]{:S(2)}, u32[]{:S(2)}) %collective-permute-start.18) | collective-permute-done | bytes 1310752 | tf_op jit(solution)/shard_map/ppermute | solution.py:511
  755.5 15.6 %z_mix.23.v_ref = bf16[32,64,16,128]{3,2,1,0:T(8,128)(2,1)} custom-call(bf16[3,64,80]{2,1,0:T(8,128)(2,1)} %select_reduce_fusion.a_ref, bf16[3,256,256]{2,1,0:T(8,128)(2,1)} %broadcast_multiply_fusion.w_ref, f32[3,1,256]{2,1,0:T(1,128)} %tile.9.b_ref, bf16[16,32,64,128]{3,2,1,0:T(8,128)(2,1)} %get-tuple-element.93.u_ref, ...), custom_call_target="tpu_custom_call" | custom-call | flops 4026531840 | bytes 29360128 | tf_op jit(solution)/shard_map/z_mix/pallas_call | solution.py:301
  771.1 17.2 %leave.4.refs_0_ = bf16[64,64,64,64]{3,2,1,0:T(8,128)(2,1)} custom-call(s32[3]{0:T(128)} %pad_add_fusion.meta, bf16[128,128]{1,0:T(8,128)(2,1)} %fusion.eye_ref, bf16[32,64,16,128]{3,2,1,0:T(8,128)(2,1)} %z_mix.23.v_ref), custom_call_target="tpu_custom_call" | custom-call | flops 2147483648 | bytes 25165824 | tf_op jit(solution)/shard_map/leave/pallas_call | solution.py:443
  788.3 15.6 %z_mix.21.v_ref = bf16[32,64,16,128]{3,2,1,0:T(8,128)(2,1)} custom-call(bf16[3,64,80]{2,1,0:T(8,128)(2,1)} %select_reduce_fusion.a_ref, bf16[3,256,256]{2,1,0:T(8,128)(2,1)} %broadcast_multiply_fusion.w_ref, f32[3,1,256]{2,1,0:T(1,128)} %tile.9.b_ref, bf16[16,32,64,128]{3,2,1,0:T(8,128)(2,1)} %get-tuple-element.85.u_ref, ...), custom_call_target="tpu_custom_call" | custom-call | flops 4026531840 | bytes 29360128 | tf_op jit(solution)/shard_map/z_mix/pallas_call | solution.py:301
  805.0 15.6 %z_mix.20.v_ref = bf16[32,64,16,128]{3,2,1,0:T(8,128)(2,1)} custom-call(bf16[3,64,80]{2,1,0:T(8,128)(2,1)} %select_reduce_fusion.a_ref, bf16[3,256,256]{2,1,0:T(8,128)(2,1)} %broadcast_multiply_fusion.w_ref, f32[3,1,256]{2,1,0:T(1,128)} %tile.9.b_ref, bf16[16,32,64,128]{3,2,1,0:T(8,128)(2,1)} %get-tuple-element.82.u_ref, ...), custom_call_target="tpu_custom_call" | custom-call | flops 4026531840 | bytes 29360128 | tf_op jit(solution)/shard_map/z_mix/pallas_call | solution.py:301
  820.6 15.6 %z_mix.22.v_ref = bf16[32,64,16,128]{3,2,1,0:T(8,128)(2,1)} custom-call(bf16[3,64,80]{2,1,0:T(8,128)(2,1)} %select_reduce_fusion.a_ref, bf16[3,256,256]{2,1,0:T(8,128)(2,1)} %broadcast_multiply_fusion.w_ref, f32[3,1,256]{2,1,0:T(1,128)} %tile.9.b_ref, bf16[16,32,64,128]{3,2,1,0:T(8,128)(2,1)} %get-tuple-element.89.u_ref, ...), custom_call_target="tpu_custom_call" | custom-call | flops 4026531840 | bytes 29360128 | tf_op jit(solution)/shard_map/z_mix/pallas_call | solution.py:301
  836.2 17.2 %leave.5.refs_0_ = bf16[64,64,64,64]{3,2,1,0:T(8,128)(2,1)} custom-call(s32[3]{0:T(128)} %pad_add_fusion.meta, bf16[128,128]{1,0:T(8,128)(2,1)} %fusion.eye_ref, bf16[32,64,16,128]{3,2,1,0:T(8,128)(2,1)} %z_mix.22.v_ref, bf16[64,64,64,64]{3,2,1,0:T(8,128)(2,1)} %leave.4.refs_0_), custom_call_target="tpu_custom_call", output_to_operand_aliasing={{}: (3, {})} | custom-call | flops 2147483648 | bytes 25165824 | tf_op jit(solution)/shard_map/leave/pallas_call | solution.py:443
  853.4 17.2 %leave.6.refs_0_ = bf16[64,64,64,64]{3,2,1,0:T(8,128)(2,1)} custom-call(s32[3]{0:T(128)} %pad_add_fusion.meta, bf16[128,128]{1,0:T(8,128)(2,1)} %fusion.eye_ref, bf16[32,64,16,128]{3,2,1,0:T(8,128)(2,1)} %z_mix.21.v_ref, bf16[64,64,64,64]{3,2,1,0:T(8,128)(2,1)} %leave.5.refs_0_), custom_call_target="tpu_custom_call", output_to_operand_aliasing={{}: (3, {})} | custom-call | flops 2147483648 | bytes 25165824 | tf_op jit(solution)/shard_map/leave/pallas_call | solution.py:443
  870.6 17.2 %leave.7 = bf16[64,64,64,64]{3,2,1,0:T(8,128)(2,1)} custom-call(s32[3]{0:T(128)} %pad_add_fusion.meta, bf16[128,128]{1,0:T(8,128)(2,1)} %fusion.eye_ref, bf16[32,64,16,128]{3,2,1,0:T(8,128)(2,1)} %z_mix.20.v_ref, bf16[64,64,64,64]{3,2,1,0:T(8,128)(2,1)} %leave.6.refs_0_), custom_call_target="tpu_custom_call", output_to_operand_aliasing={{}: (3, {})} | custom-call | flops 2147483648 | bytes 25165824 | tf_op jit(solution)/shard_map/leave/pallas_call | solution.py:443
  (139 shorter events, 304.7 us)
Async XLA Ops:
  1.2 14.3 %copy-start.14 = (f32[3,3,21]{2,1,0:T(4,128)S(1)}, f32[3,3,21]{2,1,0:T(4,128)}, u32[]{:S(2)}) copy-start(f32[3,3,21]{2,1,0:T(4,128)} %param.5) | copy-start | bytes 2272
  14.6 15.1 %collective-permute-start.8 = (bf16[32,64,16,128]{3,2,1,0:T(8,128)(2,1)}, bf16[32,64,16,128]{3,2,1,0:T(8,128)(2,1)}, u32[]{:S(2)}, u32[]{:S(2)}) collective-permute-start(bf16[32,64,16,128]{3,2,1,0:T(8,128)(2,1)} %enter.7.refs_2_.refs_1_.v_ref), channel_id=1, source_target_pairs={{0,1},{1,0},{2,3},{3,2},{4,5},{5,4},{6,7},{7,6}} | collective-permute-start | bytes 25165832 | tf_op jit(solution)/shard_map/ppermute | solution.py:496
  15.9 403.6 %copy-start.12 = (bf16[3,32,64]{2,1,0:T(8,128)(2,1)}, bf16[3,32,64]{2,1,0:T(8,128)(2,1)S(1)}, u32[]{:S(2)}) copy-start(bf16[3,32,64]{2,1,0:T(8,128)(2,1)S(1)} %select_reduce_fusion.1.a_ref) | copy-start | bytes 36868
  44.8 32.1 %collective-permute-start.9 = (bf16[32,10,16,128]{3,2,1,0:T(8,128)(2,1)}, bf16[32,10,16,128]{3,2,1,0:T(8,128)(2,1)S(1)}, u32[]{:S(2)}, u32[]{:S(2)}) collective-permute-start(bf16[32,10,16,128]{3,2,1,0:T(8,128)(2,1)} %get-tuple-element.66), channel_id=1, source_target_pairs={{0,2},{2,0},{1,3},{3,1},{4,6},{6,4},{5,7},{7,5}} | collective-permute-start | bytes 3932168 | tf_op jit(solution)/shard_map/ppermute | solution.py:511
  78.0 13.2 %copy-start.15 = (f32[3,64]{1,0:T(4,128)S(1)}, f32[3,64]{1,0:T(4,128)}, u32[]{:S(2)}) copy-start(f32[3,64]{1,0:T(4,128)} %param.7) | copy-start | bytes 2308
  78.0 14.3 %copy-start.13 = (bf16[3,64,64]{2,1,0:T(8,128)(2,1)S(1)}, bf16[3,64,64]{2,1,0:T(8,128)(2,1)}, u32[]{:S(2)}) copy-start(bf16[3,64,64]{2,1,0:T(8,128)(2,1)} %param.6) | copy-start | bytes 73732
  89.3 30.8 %collective-permute-start.10 = (bf16[16,4,10,8,128]{4,3,2,1,0:T(8,128)(2,1)}, bf16[16,4,10,8,128]{4,3,2,1,0:T(8,128)(2,1)S(1)}, u32[]{:S(2)}, u32[]{:S(2)}) collective-permute-start(bf16[16,4,10,8,128]{4,3,2,1,0:T(8,128)(2,1)} %get-tuple-element.68), channel_id=1, source_target_pairs={{0,4},{4,0},{1,5},{5,1},{2,6},{6,2},{3,7},{7,3}} | collective-permute-start | bytes 3932168 | tf_op jit(solution)/shard_map/ppermute | solution.py:514
  136.8 119.4 %collective-permute-start.15 = (bf16[32,64,16,128]{3,2,1,0:T(8,128)(2,1)}, bf16[32,64,16,128]{3,2,1,0:T(8,128)(2,1)}, u32[]{:S(2)}, u32[]{:S(2)}) collective-permute-start(bf16[32,64,16,128]{3,2,1,0:T(8,128)(2,1)} %z_mix.16.refs_3_.refs_1_.v_ref), channel_id=1, source_target_pairs={{0,1},{1,0},{2,3},{3,2},{4,5},{5,4},{6,7},{7,6}} | collective-permute-start | bytes 25165832 | tf_op jit(solution)/shard_map/ppermute | solution.py:496
  165.2 31.4 %collective-permute-start.6 = (bf16[32,10,16,128]{3,2,1,0:T(8,128)(2,1)}, bf16[32,10,16,128]{3,2,1,0:T(8,128)(2,1)S(1)}, u32[]{:S(2)}, u32[]{:S(2)}) collective-permute-start(bf16[32,10,16,128]{3,2,1,0:T(8,128)(2,1)} %get-tuple-element.62), channel_id=1, source_target_pairs={{0,2},{2,0},{1,3},{3,1},{4,6},{6,4},{5,7},{7,5}} | collective-permute-start | bytes 3932168 | tf_op jit(solution)/shard_map/ppermute | solution.py:511
  208.9 30.5 %collective-permute-start.7 = (bf16[16,4,10,8,128]{4,3,2,1,0:T(8,128)(2,1)}, bf16[16,4,10,8,128]{4,3,2,1,0:T(8,128)(2,1)S(1)}, u32[]{:S(2)}, u32[]{:S(2)}) collective-permute-start(bf16[16,4,10,8,128]{4,3,2,1,0:T(8,128)(2,1)} %get-tuple-element.64), channel_id=1, source_target_pairs={{0,4},{4,0},{1,5},{5,1},{2,6},{6,2},{3,7},{7,3}} | collective-permute-start | bytes 3932168 | tf_op jit(solution)/shard_map/ppermute | solution.py:514
  239.5 1.1 copy-start.11
  271.3 29.7 %collective-permute-start.16 = (bf16[32,10,16,128]{3,2,1,0:T(8,128)(2,1)}, bf16[32,10,16,128]{3,2,1,0:T(8,128)(2,1)S(1)}, u32[]{:S(2)}, u32[]{:S(2)}) collective-permute-start(bf16[32,10,16,128]{3,2,1,0:T(8,128)(2,1)} %get-tuple-element.77), channel_id=1, source_target_pairs={{0,2},{2,0},{1,3},{3,1},{4,6},{6,4},{5,7},{7,5}} | collective-permute-start | bytes 3932168 | tf_op jit(solution)/shard_map/ppermute | solution.py:511
  313.5 38.5 %collective-permute-start.17 = (bf16[16,4,10,8,128]{4,3,2,1,0:T(8,128)(2,1)}, bf16[16,4,10,8,128]{4,3,2,1,0:T(8,128)(2,1)}, u32[]{:S(2)}, u32[]{:S(2)}) collective-permute-start(bf16[16,4,10,8,128]{4,3,2,1,0:T(8,128)(2,1)} %get-tuple-element.79), channel_id=1, source_target_pairs={{0,4},{4,0},{1,5},{5,1},{2,6},{6,2},{3,7},{7,3}} | collective-permute-start | bytes 3932168 | tf_op jit(solution)/shard_map/ppermute | solution.py:514
  349.9 31.9 %collective-permute-start.2 = (bf16[32,10,16,128]{3,2,1,0:T(8,128)(2,1)}, bf16[32,10,16,128]{3,2,1,0:T(8,128)(2,1)S(1)}, u32[]{:S(2)}, u32[]{:S(2)}) collective-permute-start(bf16[32,10,16,128]{3,2,1,0:T(8,128)(2,1)} %get-tuple-element.54), channel_id=1, source_target_pairs={{0,2},{2,0},{1,3},{3,1},{4,6},{6,4},{5,7},{7,5}} | collective-permute-start | bytes 3932168 | tf_op jit(solution)/shard_map/ppermute | solution.py:511
  351.2 55.3 %collective-permute-start = (bf16[32,10,16,128]{3,2,1,0:T(8,128)(2,1)}, bf16[32,10,16,128]{3,2,1,0:T(8,128)(2,1)S(1)}, u32[]{:S(2)}, u32[]{:S(2)}) collective-permute-start(bf16[32,10,16,128]{3,2,1,0:T(8,128)(2,1)} %get-tuple-element.51), channel_id=1, source_target_pairs={{0,2},{2,0},{1,3},{3,1},{4,6},{6,4},{5,7},{7,5}} | collective-permute-start | bytes 3932168 | tf_op jit(solution)/shard_map/ppermute | solution.py:511
  367.6 293.6 %collective-permute-start.22 = (bf16[32,64,16,128]{3,2,1,0:T(8,128)(2,1)}, bf16[32,64,16,128]{3,2,1,0:T(8,128)(2,1)}, u32[]{:S(2)}, u32[]{:S(2)}) collective-permute-start(bf16[32,64,16,128]{3,2,1,0:T(8,128)(2,1)} %z_mix.19.refs_3_.refs_1_.v_ref), channel_id=1, source_target_pairs={{0,1},{1,0},{2,3},{3,2},{4,5},{5,4},{6,7},{7,6}} | collective-permute-start | bytes 25165832 | tf_op jit(solution)/shard_map/ppermute | solution.py:496
  394.1 26.0 %collective-permute-start.3 = (bf16[16,4,10,8,128]{4,3,2,1,0:T(8,128)(2,1)}, bf16[16,4,10,8,128]{4,3,2,1,0:T(8,128)(2,1)S(1)}, u32[]{:S(2)}, u32[]{:S(2)}) collective-permute-start(bf16[16,4,10,8,128]{4,3,2,1,0:T(8,128)(2,1)} %get-tuple-element.56), channel_id=1, source_target_pairs={{0,4},{4,0},{1,5},{5,1},{2,6},{6,2},{3,7},{7,3}} | collective-permute-start | bytes 3932168 | tf_op jit(solution)/shard_map/ppermute | solution.py:514
  419.0 27.7 %collective-permute-start.1 = (bf16[16,4,10,8,128]{4,3,2,1,0:T(8,128)(2,1)}, bf16[16,4,10,8,128]{4,3,2,1,0:T(8,128)(2,1)S(1)}, u32[]{:S(2)}, u32[]{:S(2)}) collective-permute-start(bf16[16,4,10,8,128]{4,3,2,1,0:T(8,128)(2,1)} %get-tuple-element.53), channel_id=1, source_target_pairs={{0,4},{4,0},{1,5},{5,1},{2,6},{6,2},{3,7},{7,3}} | collective-permute-start | bytes 3932168 | tf_op jit(solution)/shard_map/ppermute | solution.py:514
  476.7 30.6 %collective-permute-start.4 = (bf16[32,10,16,128]{3,2,1,0:T(8,128)(2,1)}, bf16[32,10,16,128]{3,2,1,0:T(8,128)(2,1)S(1)}, u32[]{:S(2)}, u32[]{:S(2)}) collective-permute-start(bf16[32,10,16,128]{3,2,1,0:T(8,128)(2,1)} %get-tuple-element.58), channel_id=1, source_target_pairs={{0,2},{2,0},{1,3},{3,1},{4,6},{6,4},{5,7},{7,5}} | collective-permute-start | bytes 3932168 | tf_op jit(solution)/shard_map/ppermute | solution.py:511
  501.3 34.2 %collective-permute-start.11 = (bf16[32,10,16,128]{3,2,1,0:T(8,128)(2,1)}, bf16[32,10,16,128]{3,2,1,0:T(8,128)(2,1)}, u32[]{:S(2)}, u32[]{:S(2)}) collective-permute-start(bf16[32,10,16,128]{3,2,1,0:T(8,128)(2,1)} %get-tuple-element.70), channel_id=1, source_target_pairs={{0,2},{2,0},{1,3},{3,1},{4,6},{6,4},{5,7},{7,5}} | collective-permute-start | bytes 3932168 | tf_op jit(solution)/shard_map/ppermute | solution.py:511
  502.2 57.5 %collective-permute-start.13 = (bf16[32,10,16,128]{3,2,1,0:T(8,128)(2,1)}, bf16[32,10,16,128]{3,2,1,0:T(8,128)(2,1)S(1)}, u32[]{:S(2)}, u32[]{:S(2)}) collective-permute-start(bf16[32,10,16,128]{3,2,1,0:T(8,128)(2,1)} %get-tuple-element.73), channel_id=1, source_target_pairs={{0,2},{2,0},{1,3},{3,1},{4,6},{6,4},{5,7},{7,5}} | collective-permute-start | bytes 3932168 | tf_op jit(solution)/shard_map/ppermute | solution.py:511
  519.6 53.1 %collective-permute-start.5 = (bf16[16,4,10,8,128]{4,3,2,1,0:T(8,128)(2,1)}, bf16[16,4,10,8,128]{4,3,2,1,0:T(8,128)(2,1)S(1)}, u32[]{:S(2)}, u32[]{:S(2)}) collective-permute-start(bf16[16,4,10,8,128]{4,3,2,1,0:T(8,128)(2,1)} %get-tuple-element.60), channel_id=1, source_target_pairs={{0,4},{4,0},{1,5},{5,1},{2,6},{6,2},{3,7},{7,3}} | collective-permute-start | bytes 3932168 | tf_op jit(solution)/shard_map/ppermute | solution.py:514
  546.8 42.5 %collective-permute-start.12 = (bf16[16,4,10,8,128]{4,3,2,1,0:T(8,128)(2,1)}, bf16[16,4,10,8,128]{4,3,2,1,0:T(8,128)(2,1)}, u32[]{:S(2)}, u32[]{:S(2)}) collective-permute-start(bf16[16,4,10,8,128]{4,3,2,1,0:T(8,128)(2,1)} %get-tuple-element.72), channel_id=1, source_target_pairs={{0,4},{4,0},{1,5},{5,1},{2,6},{6,2},{3,7},{7,3}} | collective-permute-start | bytes 3932168 | tf_op jit(solution)/shard_map/ppermute | solution.py:514
  572.1 47.4 %collective-permute-start.14 = (bf16[16,4,10,8,128]{4,3,2,1,0:T(8,128)(2,1)}, bf16[16,4,10,8,128]{4,3,2,1,0:T(8,128)(2,1)S(1)}, u32[]{:S(2)}, u32[]{:S(2)}) collective-permute-start(bf16[16,4,10,8,128]{4,3,2,1,0:T(8,128)(2,1)} %get-tuple-element.75), channel_id=1, source_target_pairs={{0,4},{4,0},{1,5},{5,1},{2,6},{6,2},{3,7},{7,3}} | collective-permute-start | bytes 3932168 | tf_op jit(solution)/shard_map/ppermute | solution.py:514
  618.3 58.7 %collective-permute-start.25 = (bf16[32,10,16,128]{3,2,1,0:T(8,128)(2,1)}, bf16[32,10,16,128]{3,2,1,0:T(8,128)(2,1)}, u32[]{:S(2)}, u32[]{:S(2)}) collective-permute-start(bf16[32,10,16,128]{3,2,1,0:T(8,128)(2,1)} %get-tuple-element.92), channel_id=1, source_target_pairs={{0,2},{2,0},{1,3},{3,1},{4,6},{6,4},{5,7},{7,5}} | collective-permute-start | bytes 3932168 | tf_op jit(solution)/shard_map/ppermute | solution.py:511
  659.1 32.0 %collective-permute-start.20 = (bf16[32,10,16,128]{3,2,1,0:T(8,128)(2,1)}, bf16[32,10,16,128]{3,2,1,0:T(8,128)(2,1)}, u32[]{:S(2)}, u32[]{:S(2)}) collective-permute-start(bf16[32,10,16,128]{3,2,1,0:T(8,128)(2,1)} %get-tuple-element.84), channel_id=1, source_target_pairs={{0,2},{2,0},{1,3},{3,1},{4,6},{6,4},{5,7},{7,5}} | collective-permute-start | bytes 3932168 | tf_op jit(solution)/shard_map/ppermute | solution.py:511
  660.0 59.1 %collective-permute-start.18 = (bf16[32,10,16,128]{3,2,1,0:T(8,128)(2,1)}, bf16[32,10,16,128]{3,2,1,0:T(8,128)(2,1)S(1)}, u32[]{:S(2)}, u32[]{:S(2)}) collective-permute-start(bf16[32,10,16,128]{3,2,1,0:T(8,128)(2,1)} %get-tuple-element.81), channel_id=1, source_target_pairs={{0,2},{2,0},{1,3},{3,1},{4,6},{6,4},{5,7},{7,5}} | collective-permute-start | bytes 3932168 | tf_op jit(solution)/shard_map/ppermute | solution.py:511
  676.2 65.6 %collective-permute-start.23 = (bf16[32,10,16,128]{3,2,1,0:T(8,128)(2,1)}, bf16[32,10,16,128]{3,2,1,0:T(8,128)(2,1)}, u32[]{:S(2)}, u32[]{:S(2)}) collective-permute-start(bf16[32,10,16,128]{3,2,1,0:T(8,128)(2,1)} %get-tuple-element.88), channel_id=1, source_target_pairs={{0,2},{2,0},{1,3},{3,1},{4,6},{6,4},{5,7},{7,5}} | collective-permute-start | bytes 3932168 | tf_op jit(solution)/shard_map/ppermute | solution.py:511
  688.5 66.0 %collective-permute-start.26 = (bf16[16,4,10,8,128]{4,3,2,1,0:T(8,128)(2,1)}, bf16[16,4,10,8,128]{4,3,2,1,0:T(8,128)(2,1)S(1)}, u32[]{:S(2)}, u32[]{:S(2)}) collective-permute-start(bf16[16,4,10,8,128]{4,3,2,1,0:T(8,128)(2,1)} %get-tuple-element.94), channel_id=1, source_target_pairs={{0,4},{4,0},{1,5},{5,1},{2,6},{6,2},{3,7},{7,3}} | collective-permute-start | bytes 3932168 | tf_op jit(solution)/shard_map/ppermute | solution.py:514
  702.4 85.9 %collective-permute-start.21 = (bf16[16,4,10,8,128]{4,3,2,1,0:T(8,128)(2,1)}, bf16[16,4,10,8,128]{4,3,2,1,0:T(8,128)(2,1)}, u32[]{:S(2)}, u32[]{:S(2)}) collective-permute-start(bf16[16,4,10,8,128]{4,3,2,1,0:T(8,128)(2,1)} %get-tuple-element.86), channel_id=1, source_target_pairs={{0,4},{4,0},{1,5},{5,1},{2,6},{6,2},{3,7},{7,3}} | collective-permute-start | bytes 3932168 | tf_op jit(solution)/shard_map/ppermute | solution.py:514
  731.4 72.5 %collective-permute-start.19 = (bf16[16,4,10,8,128]{4,3,2,1,0:T(8,128)(2,1)}, bf16[16,4,10,8,128]{4,3,2,1,0:T(8,128)(2,1)S(1)}, u32[]{:S(2)}, u32[]{:S(2)}) collective-permute-start(bf16[16,4,10,8,128]{4,3,2,1,0:T(8,128)(2,1)} %get-tuple-element.83), channel_id=1, source_target_pairs={{0,4},{4,0},{1,5},{5,1},{2,6},{6,2},{3,7},{7,3}} | collective-permute-start | bytes 3932168 | tf_op jit(solution)/shard_map/ppermute | solution.py:514
  753.0 67.6 %collective-permute-start.24 = (bf16[16,4,10,8,128]{4,3,2,1,0:T(8,128)(2,1)}, bf16[16,4,10,8,128]{4,3,2,1,0:T(8,128)(2,1)}, u32[]{:S(2)}, u32[]{:S(2)}) collective-permute-start(bf16[16,4,10,8,128]{4,3,2,1,0:T(8,128)(2,1)} %get-tuple-element.90), channel_id=1, source_target_pairs={{0,4},{4,0},{1,5},{5,1},{2,6},{6,2},{3,7},{7,3}} | collective-permute-start | bytes 3932168 | tf_op jit(solution)/shard_map/ppermute | solution.py:514
  (15 other events, 16.3 us)
where the time goes:
time: 897 us; the launch traced here: 888 us
  Pallas kernels  599 us (67%)
  waiting for transfers between devices  234 us (26%)
  starting transfers between devices  28.3 us (3%)
  local copies, waits for them, and re-layouts  21.1 us (2%)
    pallas_call x12, Pallas kernels, z_mix(): pl.pallas_call(functools.partial(z_kernel, half), grid=(jl_len // 8,), in...  187 us
    ppermute x12, waiting for transfers between devices, local_layers(): far_y[p + t] = (u1, t, lax.ppermute(send[t], 'y', SWAP))  170 us
    pallas_call x9, Pallas kernels, x_pass(): pl.pallas_call(functools.partial(x_kernel, n_in, half), grid_spec=pltpu.P...  154 us
    pallas_call x12, Pallas kernels, y_pass(): pl.pallas_call(functools.partial(y_kernel, half), grid_spec=pltpu.Prefetc...  136 us
    pallas_call x4, Pallas kernels, leave(): pl.pallas_call(leave_kernel, grid_spec=pltpu.PrefetchScalarGridSpec(num_s...  68.8 us
    ppermute x12, waiting for transfers between devices, local_layers(): far_z[p] = lax.ppermute(send, 'z', SWAP)  64.1 us
    pallas_call x4, Pallas kernels, enter(): pl.pallas_call(enter_kernel, grid_spec=pltpu.PrefetchScalarGridSpec(num_s...  53.3 us
  transfers between devices with their start and end apart: 27, of which 14 were waited for; matrix products, arithmetic and copies ran while one was open for 1% of the time, Pallas kernels for 51%

commit v1 on v0

--- a/solution.py
+++ b/solution.py
@@ -19,6 +19,7 @@
 LQ = 4
 EJ = 16
 EQ = 4
+VMEM_BYTES = 67_043_328
 PAD = 1
 LANES = 128
 F32 = jnp.float32
@@ -68,7 +69,7 @@
     return pltpu.roll(v, LANES // 2, 1)
 
 
-def x_kernel(n_in, half, meta, a_ref, *refs):
+def x_kernel(n_in, first_in, half, meta, a_ref, *refs):
     vols, u_ref, sends, s_ref = refs[:n_in], refs[n_in], refs[n_in + 1 : -1], refs[-1]
     jl_len, ci = vols[0].shape[0], vols[0].shape[2]
     planes = len(sends) * ci
@@ -76,7 +77,7 @@
     y_pos = meta[1]
     first = jnp.where(y_pos == 0, jl_len - half, 0)
     group = 8
-    mat = a_ref[0]
+    mat = a_ref[0][:planes, first_in * ci : (first_in + n_in) * ci]
 
     def pair(kp, slot):
         for par in range(2):
@@ -113,15 +114,15 @@
     lax.fori_loop(0, vols[0].shape[1] // (2 * XQ), body, 0)
 
 
-def x_pass(meta, mats, layer, vols, half):
+def x_pass(meta, mats, layer, vols, n_own, half):
     jl_len, k_len, ci, _ = vols[0].shape
-    n_in, n_own = len(vols), mats.shape[1] // CI
+    n_in = len(vols)
     vol_spec = pl.BlockSpec((jl_len, KB, ci, LANES), lambda s, m: (0, s, 0, 0))
     send_spec = pl.BlockSpec((KB // 2, half, ci, LANES), lambda s, m: (s, 0, 0, 0))
     send_shape = jax.ShapeDtypeStruct((k_len // 2, half, ci, LANES), BF16)
     size = jl_len * k_len * ci * LANES
     return pl.pallas_call(
-        functools.partial(x_kernel, n_in, half),
+        functools.partial(x_kernel, n_in, n_own + 2 - n_in, half),
         grid_spec=pltpu.PrefetchScalarGridSpec(
             num_scalar_prefetch=1,
             grid=(k_len // KB,),
@@ -226,15 +227,16 @@
             jax.ShapeDtypeStruct((ci, jl_len // 8, half, 8, LANES), BF16),
         ],
         cost_estimate=pl.CostEstimate(flops=size * 160 * 4, bytes_accessed=size * 5, transcendentals=0),
+        compiler_params=pltpu.CompilerParams(vmem_limit_bytes=VMEM_BYTES),
         name="y_pass",
     )(meta, mats, u1, nb)
 
 
 class Mixer:
-    def __init__(self, half, a_ref, w_ref, b_ref, u_ref, nb_ref, nb_s, u3_s):
+    def __init__(self, half, a_ref, w_ref, b_ref, u_ref, nb_ref, nb_s):
         self.ci, self.jb, self.k_len = u_ref.shape[0], u_ref.shape[1], u_ref.shape[2]
         self.half, self.a_ref, self.w_ref, self.b_ref = half, a_ref, w_ref, b_ref
-        self.u_ref, self.nb_ref, self.nb_s, self.u3_s = u_ref, nb_ref, nb_s, u3_s
+        self.u_ref, self.nb_ref, self.nb_s = u_ref, nb_ref, nb_s
         self.pitch = self.jb + PAD
         self.span = 16 * self.pitch
 
@@ -248,32 +250,31 @@
 
         lax.fori_loop(0, self.ci, one, 0)
 
-    def filt(self, jl, slot):
-        for ip in range(self.ci // 2):
+    def gelu(self, jl, ip0):
+        rows = []
+        for ip in (ip0, ip0 + 1):
             parts = []
             for i in (2 * ip, 2 * ip + 1):
                 far = self.nb_s[pl.ds(i * self.span + jl, 16, stride=self.pitch), :].astype(BF16)
                 parts.append(jnp.concatenate([self.u_ref[i, jl], far], axis=0))
             u3 = jnp.dot(self.a_ref[0], jnp.concatenate(parts, axis=1), preferred_element_type=F32)
-            self.u3_s[slot, pl.ds(ip * self.k_len, self.k_len), :] = u3.astype(BF16)
-
-    def gelu(self, ip, slot):
-        u3 = self.u3_s[slot, pl.ds(ip * self.k_len, self.k_len), :]
-        m = jnp.dot(u3, self.w_ref[0], preferred_element_type=F32) + self.b_ref[0]
+            rows.append(u3.astype(BF16))
+        m = jnp.dot(jnp.concatenate(rows, axis=0), self.w_ref[0], preferred_element_type=F32) + self.b_ref[0]
         return 0.5 * m * (1.0 + lax.erf(m * 0.7071067811865476))
 
 
-def z_kernel(half, a_ref, w_ref, b_ref, u_ref, nb_ref, v_ref, o_ref, nb_s, u3_s, g_s):
-    mixer = Mixer(half, a_ref, w_ref, b_ref, u_ref, nb_ref, nb_s, u3_s)
+def z_kernel(half, a_ref, w_ref, b_ref, u_ref, nb_ref, v_ref, o_ref, nb_s, g_s):
+    mixer = Mixer(half, a_ref, w_ref, b_ref, u_ref, nb_ref, nb_s)
     ci, k_len = mixer.ci, mixer.k_len
     row = k_len + PAD
     mixer.fill()
 
-    def mix(slot):
-        for ip in range(ci // 2):
-            g = mixer.gelu(ip, slot)
-            for t in range(2):
-                g_s[slot, pl.ds((2 * ip + t) * row, k_len), :] = g[:, t * LANES : (t + 1) * LANES]
+    def mix(jl, slot):
+        for ip in range(0, ci // 2, 2):
+            g = mixer.gelu(jl, ip)
+            for i in range(4):
+                part = g[i // 2 * k_len : (i // 2 + 1) * k_len, i % 2 * LANES : (i % 2 + 1) * LANES]
+                g_s[slot, pl.ds((2 * ip + i) * row, k_len), :] = part
 
     def finish(jl, slot):
         for k in range(k_len):
@@ -282,9 +283,7 @@
 
     def body(step, _):
         for q in range(ZQ):
-            mixer.filt(step * ZQ + q, q)
-        for q in range(ZQ):
-            mix(q)
+            mix(step * ZQ + q, q)
             if q:
                 finish(step * ZQ + q - 1, q - 1)
         finish(step * ZQ + ZQ - 1, ZQ - 1)
@@ -312,11 +311,11 @@
         out_specs=vol_spec,
         scratch_shapes=[
             pltpu.VMEM((ci * 16 * (8 + PAD), LANES), F32),
-            pltpu.VMEM((ZQ, ci // 2 * k_len, 2 * LANES), BF16),
             pltpu.VMEM((ZQ, ci * (k_len + PAD), LANES), F32),
         ],
         out_shape=jax.ShapeDtypeStruct(vol.shape, BF16),
         cost_estimate=pl.CostEstimate(flops=size * 160 * 6, bytes_accessed=size * 7, transcendentals=size),
+        compiler_params=pltpu.CompilerParams(vmem_limit_bytes=VMEM_BYTES),
         name="z_mix",
     )(mats, w4, bias, u2, nb, vol)
 
@@ -465,11 +464,11 @@
 
 SWAP = [(0, 1), (1, 0)]
 ORDER = (
-    "e3", "e2", "e1", "x031", "e0", "x021", "y03", "x002", "y02", "z03",
-    "y00", "z02", "y01", "x131", "z00", "z01", "x101", "y13", "x112", "y10",
-    "z13", "y11", "z10", "y12", "z11", "x201", "z12", "x231", "y20", "x212",
-    "y23", "z20", "l0", "y21", "y22", "z23", "l3", "z21", "z22", "l2",
-    "l1",
+    "e2", "e1", "e3", "x021", "x031", "e0", "y02", "x002", "y03", "z02",
+    "y00", "z03", "y01", "z00", "x131", "z01", "x102", "y13", "x121", "y10",
+    "z13", "y11", "z10", "y12", "z11", "x201", "z12", "x211", "y20", "x222",
+    "y21", "z20", "l0", "y22", "z21", "y23", "l1", "z22", "z23", "l3",
+    "l2",
 )
 
 
@@ -504,9 +503,7 @@
                 n_own = int(op[3])
                 own = [vols[layer, q] for q in range(max(p - 1, 0), p + n_own)]
                 after = vols[layer, p + n_own] if p + n_own < n_chunks else beyond[layer]
-                first = 0 if p else CI
-                mats = mats_x[:, : n_own * CI, first : (n_own + 2) * CI]
-                u1, *send = x_pass(meta, mats, layer, own + [after], half)
+                u1, *send = x_pass(meta, mats_x, layer, own + [after], n_own, half)
                 for t in range(n_own):
                     far_y[p + t] = (u1, t, lax.ppermute(send[t], "y", SWAP))
             elif kind == "y":

time: 897 us -> 860 us (0.959)
  local copies, waits for them, and re-layouts: 21.1 us -> 3.89 us
  Pallas kernels: 599 us -> 584 us
    unnamed x43 -> x5, local copies, waits for them, and re-layouts: 17.4 us -> 0.68 us
    pallas_call x12, Pallas kernels: 187 us -> 170 us  [z_mix(): pl.pallas_call(functools.partial(z_kernel, half), grid=(jl_len // 8,), in...]
  transfers between devices with their start and end apart: 27 -> 27, of which waited for: 14 -> 12; matrix products, arithmetic and copies ran while one was open for 1% -> 1% of each run, Pallas kernels for 51% -> 56%
where the time goes in v1:
time: 860 us; the launch traced here: 850 us
  Pallas kernels  584 us (68%)
  waiting for transfers between devices  230 us (27%)
  starting transfers between devices  26.4 us (3%)
    pallas_call x12, Pallas kernels, z_mix(): pl.pallas_call(functools.partial(z_kernel, half), grid=(jl_len // 8,), in...  170 us
    ppermute x12, waiting for transfers between devices, local_layers(): far_y[p + t] = (u1, t, lax.ppermute(send[t], 'y', SWAP))  164 us
    pallas_call x9, Pallas kernels, x_pass(): pl.pallas_call(functools.partial(x_kernel, n_in, n_own + 2 - n_in, half),...  155 us
    pallas_call x12, Pallas kernels, y_pass(): pl.pallas_call(functools.partial(y_kernel, half), grid_spec=pltpu.Prefetc...  136 us
    pallas_call x4, Pallas kernels, leave(): pl.pallas_call(leave_kernel, grid_spec=pltpu.PrefetchScalarGridSpec(num_s...  68.8 us
    ppermute x12, waiting for transfers between devices, local_layers(): far_z[p] = lax.ppermute(send, 'z', SWAP)  65.5 us
    pallas_call x4, Pallas kernels, enter(): pl.pallas_call(enter_kernel, grid_spec=pltpu.PrefetchScalarGridSpec(num_s...  53.4 us
  transfers between devices with their start and end apart: 27, of which 12 were waited for; matrix products, arithmetic and copies ran while one was open for 1% of the time, Pallas kernels for 56%

profile of v1, /device:TPU:0, one launch (start us, length us, event | category | flops | bytes accessed | tf_op | source)
XLA Modules:
  0.0 850.1 jit_solution(15621135260712582055)
XLA Ops:
  30.4 15.0 %x_pass.12 = (bf16[16,64,32,128]{3,2,1,0:T(8,128)(2,1)}, bf16[32,10,16,128]{3,2,1,0:T(8,128)(2,1)}) custom-call(s32[3]{0:T(128)} %pad_add_fusion.meta, bf16[3,32,64]{2,1,0:T(8,128)(2,1)} %select_reduce_fusion.1.a_ref, bf16[32,64,16,128]{3,2,1,0:T(8,128)(2,1)} %enter.6.refs_2_.refs_1_.v_ref.refs_0_, bf16[32,64,16,128]{3,2,1,0:T(8,128)(2,1)} %enter.7.refs_2_.refs_1_.v_ref, ...), custom_call_target="tpu_custom_call" | custom-call | flops 2147483648 | bytes 33554432 | tf_op jit(solution)/shard_map/x_pass/pallas_call | solution.py:124
  48.8 28.8 %collective-permute-done.9.nb_ref = bf16[32,10,16,128]{3,2,1,0:T(8,128)(2,1)} collective-permute-done((bf16[32,10,16,128]{3,2,1,0:T(8,128)(2,1)}, bf16[32,10,16,128]{3,2,1,0:T(8,128)(2,1)}, u32[]{:S(2)}, u32[]{:S(2)}) %collective-permute-start.9) | collective-permute-done | bytes 1310752 | tf_op jit(solution)/shard_map/ppermute | solution.py:508
  96.5 23.3 %collective-permute-done.10.nb_ref = bf16[16,4,10,8,128]{4,3,2,1,0:T(8,128)(2,1)} collective-permute-done((bf16[16,4,10,8,128]{4,3,2,1,0:T(8,128)(2,1)}, bf16[16,4,10,8,128]{4,3,2,1,0:T(8,128)(2,1)}, u32[]{:S(2)}, u32[]{:S(2)}) %collective-permute-start.10) | collective-permute-done | bytes 1310752 | tf_op jit(solution)/shard_map/ppermute | solution.py:511
  119.8 14.2 %z_mix.16.refs_2_.refs_1_.v_ref = bf16[32,64,16,128]{3,2,1,0:T(8,128)(2,1)} custom-call(bf16[3,64,80]{2,1,0:T(8,128)(2,1)} %select_reduce_fusion.a_ref, bf16[3,256,256]{2,1,0:T(8,128)(2,1)} %broadcast_multiply_fusion.w_ref, f32[3,1,256]{2,1,0:T(1,128)} %tile.9.b_ref, bf16[16,32,64,128]{3,2,1,0:T(8,128)(2,1)} %get-tuple-element.67.u_ref, ...), custom_call_target="tpu_custom_call" | custom-call | flops 4026531840 | bytes 29360128 | tf_op jit(solution)/shard_map/z_mix/pallas_call | solution.py:300
  147.2 14.9 %x_pass.10 = (bf16[16,64,32,128]{3,2,1,0:T(8,128)(2,1)}, bf16[32,10,16,128]{3,2,1,0:T(8,128)(2,1)}) custom-call(s32[3]{0:T(128)} %pad_add_fusion.meta, bf16[3,32,64]{2,1,0:T(8,128)(2,1)} %select_reduce_fusion.1.a_ref, bf16[32,64,16,128]{3,2,1,0:T(8,128)(2,1)} %enter.5.refs_1_.v_ref.refs_0_, bf16[32,64,16,128]{3,2,1,0:T(8,128)(2,1)} %enter.6.refs_2_.refs_1_.v_ref.refs_0_, ...), custom_call_target="tpu_custom_call" | custom-call | flops 2147483648 | bytes 33554432 | tf_op jit(solution)/shard_map/x_pass/pallas_call | solution.py:124
  163.6 30.1 %collective-permute-done.4.nb_ref = bf16[32,10,16,128]{3,2,1,0:T(8,128)(2,1)} collective-permute-done((bf16[32,10,16,128]{3,2,1,0:T(8,128)(2,1)}, bf16[32,10,16,128]{3,2,1,0:T(8,128)(2,1)}, u32[]{:S(2)}, u32[]{:S(2)}) %collective-permute-start.4) | collective-permute-done | bytes 1310752 | tf_op jit(solution)/shard_map/ppermute | solution.py:508
  206.4 29.2 %collective-permute-done.5.nb_ref = bf16[16,4,10,8,128]{4,3,2,1,0:T(8,128)(2,1)} collective-permute-done((bf16[16,4,10,8,128]{4,3,2,1,0:T(8,128)(2,1)}, bf16[16,4,10,8,128]{4,3,2,1,0:T(8,128)(2,1)}, u32[]{:S(2)}, u32[]{:S(2)}) %collective-permute-start.5) | collective-permute-done | bytes 1310752 | tf_op jit(solution)/shard_map/ppermute | solution.py:511
  235.5 14.1 %z_mix.14.refs_2_.refs_1_.v_ref.refs_0_ = bf16[32,64,16,128]{3,2,1,0:T(8,128)(2,1)} custom-call(bf16[3,64,80]{2,1,0:T(8,128)(2,1)} %select_reduce_fusion.a_ref, bf16[3,256,256]{2,1,0:T(8,128)(2,1)} %broadcast_multiply_fusion.w_ref, f32[3,1,256]{2,1,0:T(1,128)} %tile.9.b_ref, bf16[16,32,64,128]{3,2,1,0:T(8,128)(2,1)} %get-tuple-element.59.u_ref, ...), custom_call_target="tpu_custom_call" | custom-call | flops 4026531840 | bytes 29360128 | tf_op jit(solution)/shard_map/z_mix/pallas_call | solution.py:300
  249.7 14.9 %x_pass.14 = (bf16[16,64,32,128]{3,2,1,0:T(8,128)(2,1)}, bf16[32,10,16,128]{3,2,1,0:T(8,128)(2,1)}) custom-call(s32[3]{0:T(128)} %pad_add_fusion.meta, bf16[3,32,64]{2,1,0:T(8,128)(2,1)} %select_reduce_fusion.1.a_ref, bf16[32,64,16,128]{3,2,1,0:T(8,128)(2,1)} %z_mix.14.refs_2_.refs_1_.v_ref.refs_0_, bf16[32,64,16,128]{3,2,1,0:T(8,128)(2,1)} %z_mix.16.refs_2_.refs_1_.v_ref, ...), custom_call_target="tpu_custom_call" | custom-call | flops 2147483648 | bytes 33554432 | tf_op jit(solution)/shard_map/x_pass/pallas_call | solution.py:124
  266.0 28.4 %collective-permute-done.14.nb_ref = bf16[32,10,16,128]{3,2,1,0:T(8,128)(2,1)} collective-permute-done((bf16[32,10,16,128]{3,2,1,0:T(8,128)(2,1)}, bf16[32,10,16,128]{3,2,1,0:T(8,128)(2,1)}, u32[]{:S(2)}, u32[]{:S(2)}) %collective-permute-start.14) | collective-permute-done | bytes 1310752 | tf_op jit(solution)/shard_map/ppermute | solution.py:508
  321.0 21.9 %x_pass.9 = (bf16[32,64,32,128]{3,2,1,0:T(8,128)(2,1)}, bf16[32,10,16,128]{3,2,1,0:T(8,128)(2,1)}, bf16[32,10,16,128]{3,2,1,0:T(8,128)(2,1)}) custom-call(s32[3]{0:T(128)} %pad_add_fusion.meta, bf16[3,32,64]{2,1,0:T(8,128)(2,1)} %select_reduce_fusion.1.a_ref, bf16[32,64,16,128]{3,2,1,0:T(8,128)(2,1)} %enter.4.refs_0_.v_ref, ...), custom_call_target="tpu_custom_call" | custom-call | flops 4294967296 | bytes 41943040 | tf_op jit(solution)/shard_map/x_pass/pallas_call | solution.py:124
  344.9 14.2 %z_mix.18.refs_2_.v_ref = bf16[32,64,16,128]{3,2,1,0:T(8,128)(2,1)} custom-call(bf16[3,64,80]{2,1,0:T(8,128)(2,1)} %select_reduce_fusion.a_ref, bf16[3,256,256]{2,1,0:T(8,128)(2,1)} %broadcast_multiply_fusion.w_ref, f32[3,1,256]{2,1,0:T(1,128)} %tile.9.b_ref, bf16[16,32,64,128]{3,2,1,0:T(8,128)(2,1)} %get-tuple-element.75.u_ref, ...), custom_call_target="tpu_custom_call" | custom-call | flops 4026531840 | bytes 29360128 | tf_op jit(solution)/shard_map/z_mix/pallas_call | solution.py:300
  359.2 15.7 %collective-permute-done.2.nb_ref = bf16[32,10,16,128]{3,2,1,0:T(8,128)(2,1)} collective-permute-done((bf16[32,10,16,128]{3,2,1,0:T(8,128)(2,1)}, bf16[32,10,16,128]{3,2,1,0:T(8,128)(2,1)}, u32[]{:S(2)}, u32[]{:S(2)}) %collective-permute-start.2) | collective-permute-done | bytes 1310752 | tf_op jit(solution)/shard_map/ppermute | solution.py:508
  411.5 14.2 %z_mix.13.refs_1_.v_ref.refs_0_ = bf16[32,64,16,128]{3,2,1,0:T(8,128)(2,1)} custom-call(bf16[3,64,80]{2,1,0:T(8,128)(2,1)} %select_reduce_fusion.a_ref, bf16[3,256,256]{2,1,0:T(8,128)(2,1)} %broadcast_multiply_fusion.w_ref, f32[3,1,256]{2,1,0:T(1,128)} %tile.9.b_ref, bf16[16,32,64,128]{3,2,1,0:T(8,128)(2,1)} %get-tuple-element.55.u_ref, ...), custom_call_target="tpu_custom_call" | custom-call | flops 4026531840 | bytes 29360128 | tf_op jit(solution)/shard_map/z_mix/pallas_call | solution.py:300
  438.7 14.2 %z_mix.12.refs_0_.v_ref = bf16[32,64,16,128]{3,2,1,0:T(8,128)(2,1)} custom-call(bf16[3,64,80]{2,1,0:T(8,128)(2,1)} %select_reduce_fusion.a_ref, bf16[3,256,256]{2,1,0:T(8,128)(2,1)} %broadcast_multiply_fusion.w_ref, f32[3,1,256]{2,1,0:T(1,128)} %tile.9.b_ref, bf16[16,32,64,128]{3,2,1,0:T(8,128)(2,1)} %get-tuple-element.52.u_ref, ...), custom_call_target="tpu_custom_call" | custom-call | flops 4026531840 | bytes 29360128 | tf_op jit(solution)/shard_map/z_mix/pallas_call | solution.py:300
  452.9 21.9 %x_pass.11 = (bf16[32,64,32,128]{3,2,1,0:T(8,128)(2,1)}, bf16[32,10,16,128]{3,2,1,0:T(8,128)(2,1)}, bf16[32,10,16,128]{3,2,1,0:T(8,128)(2,1)}) custom-call(s32[3]{0:T(128)} %pad_add_fusion.meta, bf16[3,32,64]{2,1,0:T(8,128)(2,1)} %select_reduce_fusion.1.a_ref, bf16[32,64,16,128]{3,2,1,0:T(8,128)(2,1)} %z_mix.12.refs_0_.v_ref, ...), custom_call_target="tpu_custom_call" | custom-call | flops 4294967296 | bytes 41943040 | tf_op jit(solution)/shard_map/x_pass/pallas_call | solution.py:124
  476.9 15.0 %x_pass.13 = (bf16[16,64,32,128]{3,2,1,0:T(8,128)(2,1)}, bf16[32,10,16,128]{3,2,1,0:T(8,128)(2,1)}) custom-call(s32[3]{0:T(128)} %pad_add_fusion.meta, bf16[3,32,64]{2,1,0:T(8,128)(2,1)} %select_reduce_fusion.1.a_ref, bf16[32,64,16,128]{3,2,1,0:T(8,128)(2,1)} %z_mix.13.refs_1_.v_ref.refs_0_, bf16[32,64,16,128]{3,2,1,0:T(8,128)(2,1)} %z_mix.14.refs_2_.refs_1_.v_ref.refs_0_, ...), custom_call_target="tpu_custom_call" | custom-call | flops 2147483648 | bytes 33554432 | tf_op jit(solution)/shard_map/x_pass/pallas_call | solution.py:124
  492.7 14.0 %collective-permute-done.21.nb_ref = bf16[32,10,16,128]{3,2,1,0:T(8,128)(2,1)} collective-permute-done((bf16[32,10,16,128]{3,2,1,0:T(8,128)(2,1)}, bf16[32,10,16,128]{3,2,1,0:T(8,128)(2,1)}, u32[]{:S(2)}, u32[]{:S(2)}) %collective-permute-start.21) | collective-permute-done | bytes 1310752 | tf_op jit(solution)/shard_map/ppermute | solution.py:508
  518.8 16.1 %collective-permute-done.6.nb_ref = bf16[32,10,16,128]{3,2,1,0:T(8,128)(2,1)} collective-permute-done((bf16[32,10,16,128]{3,2,1,0:T(8,128)(2,1)}, bf16[32,10,16,128]{3,2,1,0:T(8,128)(2,1)}, u32[]{:S(2)}, u32[]{:S(2)}) %collective-permute-start.6) | collective-permute-done | bytes 1310752 | tf_op jit(solution)/shard_map/ppermute | solution.py:508
  569.6 14.2 %z_mix.21.refs_0_.v_ref = bf16[32,64,16,128]{3,2,1,0:T(8,128)(2,1)} custom-call(bf16[3,64,80]{2,1,0:T(8,128)(2,1)} %select_reduce_fusion.a_ref, bf16[3,256,256]{2,1,0:T(8,128)(2,1)} %broadcast_multiply_fusion.w_ref, f32[3,1,256]{2,1,0:T(1,128)} %tile.9.b_ref, bf16[16,32,64,128]{3,2,1,0:T(8,128)(2,1)} %get-tuple-element.85.u_ref, ...), custom_call_target="tpu_custom_call" | custom-call | flops 4026531840 | bytes 29360128 | tf_op jit(solution)/shard_map/z_mix/pallas_call | solution.py:300
  583.8 14.2 %z_mix.15.refs_0_.refs_1_.v_ref = bf16[32,64,16,128]{3,2,1,0:T(8,128)(2,1)} custom-call(bf16[3,64,80]{2,1,0:T(8,128)(2,1)} %select_reduce_fusion.a_ref, bf16[3,256,256]{2,1,0:T(8,128)(2,1)} %broadcast_multiply_fusion.w_ref, f32[3,1,256]{2,1,0:T(1,128)} %tile.9.b_ref, bf16[16,32,64,128]{3,2,1,0:T(8,128)(2,1)} %get-tuple-element.63.u_ref, ...), custom_call_target="tpu_custom_call" | custom-call | flops 4026531840 | bytes 29360128 | tf_op jit(solution)/shard_map/z_mix/pallas_call | solution.py:300
  612.8 14.2 %z_mix.17.refs_1_.v_ref.refs_2_ = bf16[32,64,16,128]{3,2,1,0:T(8,128)(2,1)} custom-call(bf16[3,64,80]{2,1,0:T(8,128)(2,1)} %select_reduce_fusion.a_ref, bf16[3,256,256]{2,1,0:T(8,128)(2,1)} %broadcast_multiply_fusion.w_ref, f32[3,1,256]{2,1,0:T(1,128)} %tile.9.b_ref, bf16[16,32,64,128]{3,2,1,0:T(8,128)(2,1)} %get-tuple-element.71.u_ref, ...), custom_call_target="tpu_custom_call" | custom-call | flops 4026531840 | bytes 29360128 | tf_op jit(solution)/shard_map/z_mix/pallas_call | solution.py:300
  626.9 15.0 %x_pass.16 = (bf16[16,64,32,128]{3,2,1,0:T(8,128)(2,1)}, bf16[32,10,16,128]{3,2,1,0:T(8,128)(2,1)}) custom-call(s32[3]{0:T(128)} %pad_add_fusion.meta, bf16[3,32,64]{2,1,0:T(8,128)(2,1)} %select_reduce_fusion.1.a_ref, bf16[32,64,16,128]{3,2,1,0:T(8,128)(2,1)} %z_mix.21.refs_0_.v_ref, bf16[32,64,16,128]{3,2,1,0:T(8,128)(2,1)} %z_mix.15.refs_0_.refs_1_.v_ref, ...), custom_call_target="tpu_custom_call" | custom-call | flops 2147483648 | bytes 33554432 | tf_op jit(solution)/shard_map/x_pass/pallas_call | solution.py:124
  643.0 23.0 %x_pass.15 = (bf16[32,64,32,128]{3,2,1,0:T(8,128)(2,1)}, bf16[32,10,16,128]{3,2,1,0:T(8,128)(2,1)}, bf16[32,10,16,128]{3,2,1,0:T(8,128)(2,1)}) custom-call(s32[3]{0:T(128)} %pad_add_fusion.meta, bf16[3,32,64]{2,1,0:T(8,128)(2,1)} %select_reduce_fusion.1.a_ref, bf16[32,64,16,128]{3,2,1,0:T(8,128)(2,1)} %z_mix.15.refs_0_.refs_1_.v_ref, ...), custom_call_target="tpu_custom_call" | custom-call | flops 4294967296 | bytes 50331648 | tf_op jit(solution)/shard_map/x_pass/pallas_call | solution.py:124
  712.4 14.2 %z_mix.23.v_ref = bf16[32,64,16,128]{3,2,1,0:T(8,128)(2,1)} custom-call(bf16[3,64,80]{2,1,0:T(8,128)(2,1)} %select_reduce_fusion.a_ref, bf16[3,256,256]{2,1,0:T(8,128)(2,1)} %broadcast_multiply_fusion.w_ref, f32[3,1,256]{2,1,0:T(1,128)} %tile.9.b_ref, bf16[16,32,64,128]{3,2,1,0:T(8,128)(2,1)} %get-tuple-element.93.u_ref, ...), custom_call_target="tpu_custom_call" | custom-call | flops 4026531840 | bytes 29360128 | tf_op jit(solution)/shard_map/z_mix/pallas_call | solution.py:300
  738.4 17.2 %leave.4.refs_0_ = bf16[64,64,64,64]{3,2,1,0:T(8,128)(2,1)} custom-call(s32[3]{0:T(128)} %pad_add_fusion.meta, bf16[128,128]{1,0:T(8,128)(2,1)} %fusion.eye_ref, bf16[32,64,16,128]{3,2,1,0:T(8,128)(2,1)} %z_mix.23.v_ref), custom_call_target="tpu_custom_call" | custom-call | flops 2147483648 | bytes 25165824 | tf_op jit(solution)/shard_map/leave/pallas_call | solution.py:442
  755.6 14.2 %z_mix.22.v_ref = bf16[32,64,16,128]{3,2,1,0:T(8,128)(2,1)} custom-call(bf16[3,64,80]{2,1,0:T(8,128)(2,1)} %select_reduce_fusion.a_ref, bf16[3,256,256]{2,1,0:T(8,128)(2,1)} %broadcast_multiply_fusion.w_ref, f32[3,1,256]{2,1,0:T(1,128)} %tile.9.b_ref, bf16[16,32,64,128]{3,2,1,0:T(8,128)(2,1)} %get-tuple-element.89.u_ref, ...), custom_call_target="tpu_custom_call" | custom-call | flops 4026531840 | bytes 29360128 | tf_op jit(solution)/shard_map/z_mix/pallas_call | solution.py:300
  769.8 17.2 %leave.5.refs_0_ = bf16[64,64,64,64]{3,2,1,0:T(8,128)(2,1)} custom-call(s32[3]{0:T(128)} %pad_add_fusion.meta, bf16[128,128]{1,0:T(8,128)(2,1)} %fusion.eye_ref, bf16[32,64,16,128]{3,2,1,0:T(8,128)(2,1)} %z_mix.22.v_ref, bf16[64,64,64,64]{3,2,1,0:T(8,128)(2,1)} %leave.4.refs_0_), custom_call_target="tpu_custom_call", output_to_operand_aliasing={{}: (3, {})} | custom-call | flops 2147483648 | bytes 25165824 | tf_op jit(solution)/shard_map/leave/pallas_call | solution.py:442
  787.0 14.2 %z_mix.20.v_ref = bf16[32,64,16,128]{3,2,1,0:T(8,128)(2,1)} custom-call(bf16[3,64,80]{2,1,0:T(8,128)(2,1)} %select_reduce_fusion.a_ref, bf16[3,256,256]{2,1,0:T(8,128)(2,1)} %broadcast_multiply_fusion.w_ref, f32[3,1,256]{2,1,0:T(1,128)} %tile.9.b_ref, bf16[16,32,64,128]{3,2,1,0:T(8,128)(2,1)} %get-tuple-element.82.u_ref, ...), custom_call_target="tpu_custom_call" | custom-call | flops 4026531840 | bytes 29360128 | tf_op jit(solution)/shard_map/z_mix/pallas_call | solution.py:300
  801.3 17.2 %leave.6.refs_0_ = bf16[64,64,64,64]{3,2,1,0:T(8,128)(2,1)} custom-call(s32[3]{0:T(128)} %pad_add_fusion.meta, bf16[128,128]{1,0:T(8,128)(2,1)} %fusion.eye_ref, bf16[32,64,16,128]{3,2,1,0:T(8,128)(2,1)} %z_mix.20.v_ref, bf16[64,64,64,64]{3,2,1,0:T(8,128)(2,1)} %leave.5.refs_0_), custom_call_target="tpu_custom_call", output_to_operand_aliasing={{}: (3, {})} | custom-call | flops 2147483648 | bytes 25165824 | tf_op jit(solution)/shard_map/leave/pallas_call | solution.py:442
  818.4 14.2 %z_mix.19.v_ref = bf16[32,64,16,128]{3,2,1,0:T(8,128)(2,1)} custom-call(bf16[3,64,80]{2,1,0:T(8,128)(2,1)} %select_reduce_fusion.a_ref, bf16[3,256,256]{2,1,0:T(8,128)(2,1)} %broadcast_multiply_fusion.w_ref, f32[3,1,256]{2,1,0:T(1,128)} %tile.9.b_ref, bf16[16,32,64,128]{3,2,1,0:T(8,128)(2,1)} %get-tuple-element.79.u_ref, ...), custom_call_target="tpu_custom_call" | custom-call | flops 4026531840 | bytes 29360128 | tf_op jit(solution)/shard_map/z_mix/pallas_call | solution.py:300
  832.7 17.2 %leave.7 = bf16[64,64,64,64]{3,2,1,0:T(8,128)(2,1)} custom-call(s32[3]{0:T(128)} %pad_add_fusion.meta, bf16[128,128]{1,0:T(8,128)(2,1)} %fusion.eye_ref, bf16[32,64,16,128]{3,2,1,0:T(8,128)(2,1)} %z_mix.19.v_ref, bf16[64,64,64,64]{3,2,1,0:T(8,128)(2,1)} %leave.6.refs_0_), custom_call_target="tpu_custom_call", output_to_operand_aliasing={{}: (3, {})} | custom-call | flops 2147483648 | bytes 25165824 | tf_op jit(solution)/shard_map/leave/pallas_call | solution.py:442
  (98 shorter events, 283.5 us)
Async XLA Ops:
  1.3 14.3 %copy-start = (f32[3,3,21]{2,1,0:T(4,128)S(1)}, f32[3,3,21]{2,1,0:T(4,128)}, u32[]{:S(2)}) copy-start(f32[3,3,21]{2,1,0:T(4,128)} %param.5) | copy-start | bytes 2272
  14.7 15.7 %collective-permute-start.8 = (bf16[32,64,16,128]{3,2,1,0:T(8,128)(2,1)}, bf16[32,64,16,128]{3,2,1,0:T(8,128)(2,1)}, u32[]{:S(2)}, u32[]{:S(2)}) collective-permute-start(bf16[32,64,16,128]{3,2,1,0:T(8,128)(2,1)} %enter.7.refs_2_.refs_1_.v_ref), channel_id=1, source_target_pairs={{0,1},{1,0},{2,3},{3,2},{4,5},{5,4},{6,7},{7,6}} | collective-permute-start | bytes 25165832 | tf_op jit(solution)/shard_map/ppermute | solution.py:495
  45.4 32.2 %collective-permute-start.9 = (bf16[32,10,16,128]{3,2,1,0:T(8,128)(2,1)}, bf16[32,10,16,128]{3,2,1,0:T(8,128)(2,1)}, u32[]{:S(2)}, u32[]{:S(2)}) collective-permute-start(bf16[32,10,16,128]{3,2,1,0:T(8,128)(2,1)} %get-tuple-element.66), channel_id=1, source_target_pairs={{0,2},{2,0},{1,3},{3,1},{4,6},{6,4},{5,7},{7,5}} | collective-permute-start | bytes 3932168 | tf_op jit(solution)/shard_map/ppermute | solution.py:508
  88.8 31.0 %collective-permute-start.10 = (bf16[16,4,10,8,128]{4,3,2,1,0:T(8,128)(2,1)}, bf16[16,4,10,8,128]{4,3,2,1,0:T(8,128)(2,1)}, u32[]{:S(2)}, u32[]{:S(2)}) collective-permute-start(bf16[16,4,10,8,128]{4,3,2,1,0:T(8,128)(2,1)} %get-tuple-element.68), channel_id=1, source_target_pairs={{0,4},{4,0},{1,5},{5,1},{2,6},{6,2},{3,7},{7,3}} | collective-permute-start | bytes 3932168 | tf_op jit(solution)/shard_map/ppermute | solution.py:511
  133.9 115.8 %collective-permute-start.13 = (bf16[32,64,16,128]{3,2,1,0:T(8,128)(2,1)}, bf16[32,64,16,128]{3,2,1,0:T(8,128)(2,1)}, u32[]{:S(2)}, u32[]{:S(2)}) collective-permute-start(bf16[32,64,16,128]{3,2,1,0:T(8,128)(2,1)} %z_mix.16.refs_2_.refs_1_.v_ref), channel_id=1, source_target_pairs={{0,1},{1,0},{2,3},{3,2},{4,5},{5,4},{6,7},{7,6}} | collective-permute-start | bytes 25165832 | tf_op jit(solution)/shard_map/ppermute | solution.py:495
  162.2 31.5 %collective-permute-start.4 = (bf16[32,10,16,128]{3,2,1,0:T(8,128)(2,1)}, bf16[32,10,16,128]{3,2,1,0:T(8,128)(2,1)}, u32[]{:S(2)}, u32[]{:S(2)}) collective-permute-start(bf16[32,10,16,128]{3,2,1,0:T(8,128)(2,1)} %get-tuple-element.58), channel_id=1, source_target_pairs={{0,2},{2,0},{1,3},{3,1},{4,6},{6,4},{5,7},{7,5}} | collective-permute-start | bytes 3932168 | tf_op jit(solution)/shard_map/ppermute | solution.py:508
  204.9 30.7 %collective-permute-start.5 = (bf16[16,4,10,8,128]{4,3,2,1,0:T(8,128)(2,1)}, bf16[16,4,10,8,128]{4,3,2,1,0:T(8,128)(2,1)}, u32[]{:S(2)}, u32[]{:S(2)}) collective-permute-start(bf16[16,4,10,8,128]{4,3,2,1,0:T(8,128)(2,1)} %get-tuple-element.60), channel_id=1, source_target_pairs={{0,4},{4,0},{1,5},{5,1},{2,6},{6,2},{3,7},{7,3}} | collective-permute-start | bytes 3932168 | tf_op jit(solution)/shard_map/ppermute | solution.py:511
  264.6 29.8 %collective-permute-start.14 = (bf16[32,10,16,128]{3,2,1,0:T(8,128)(2,1)}, bf16[32,10,16,128]{3,2,1,0:T(8,128)(2,1)}, u32[]{:S(2)}, u32[]{:S(2)}) collective-permute-start(bf16[32,10,16,128]{3,2,1,0:T(8,128)(2,1)} %get-tuple-element.74), channel_id=1, source_target_pairs={{0,2},{2,0},{1,3},{3,1},{4,6},{6,4},{5,7},{7,5}} | collective-permute-start | bytes 3932168 | tf_op jit(solution)/shard_map/ppermute | solution.py:508
  306.2 38.7 %collective-permute-start.15 = (bf16[16,4,10,8,128]{4,3,2,1,0:T(8,128)(2,1)}, bf16[16,4,10,8,128]{4,3,2,1,0:T(8,128)(2,1)}, u32[]{:S(2)}, u32[]{:S(2)}) collective-permute-start(bf16[16,4,10,8,128]{4,3,2,1,0:T(8,128)(2,1)} %get-tuple-element.76), channel_id=1, source_target_pairs={{0,4},{4,0},{1,5},{5,1},{2,6},{6,2},{3,7},{7,3}} | collective-permute-start | bytes 3932168 | tf_op jit(solution)/shard_map/ppermute | solution.py:511
  342.9 32.0 %collective-permute-start.2 = (bf16[32,10,16,128]{3,2,1,0:T(8,128)(2,1)}, bf16[32,10,16,128]{3,2,1,0:T(8,128)(2,1)}, u32[]{:S(2)}, u32[]{:S(2)}) collective-permute-start(bf16[32,10,16,128]{3,2,1,0:T(8,128)(2,1)} %get-tuple-element.54), channel_id=1, source_target_pairs={{0,2},{2,0},{1,3},{3,1},{4,6},{6,4},{5,7},{7,5}} | collective-permute-start | bytes 3932168 | tf_op jit(solution)/shard_map/ppermute | solution.py:508
  344.1 55.5 %collective-permute-start = (bf16[32,10,16,128]{3,2,1,0:T(8,128)(2,1)}, bf16[32,10,16,128]{3,2,1,0:T(8,128)(2,1)}, u32[]{:S(2)}, u32[]{:S(2)}) collective-permute-start(bf16[32,10,16,128]{3,2,1,0:T(8,128)(2,1)} %get-tuple-element.51), channel_id=1, source_target_pairs={{0,2},{2,0},{1,3},{3,1},{4,6},{6,4},{5,7},{7,5}} | collective-permute-start | bytes 3932168 | tf_op jit(solution)/shard_map/ppermute | solution.py:508
  359.2 283.8 %collective-permute-start.16 = (bf16[32,64,16,128]{3,2,1,0:T(8,128)(2,1)}, bf16[32,64,16,128]{3,2,1,0:T(8,128)(2,1)}, u32[]{:S(2)}, u32[]{:S(2)}) collective-permute-start(bf16[32,64,16,128]{3,2,1,0:T(8,128)(2,1)} %z_mix.18.refs_2_.v_ref), channel_id=1, source_target_pairs={{0,1},{1,0},{2,3},{3,2},{4,5},{5,4},{6,7},{7,6}} | collective-permute-start | bytes 25165832 | tf_op jit(solution)/shard_map/ppermute | solution.py:495
  386.1 25.3 %collective-permute-start.3 = (bf16[16,4,10,8,128]{4,3,2,1,0:T(8,128)(2,1)}, bf16[16,4,10,8,128]{4,3,2,1,0:T(8,128)(2,1)}, u32[]{:S(2)}, u32[]{:S(2)}) collective-permute-start(bf16[16,4,10,8,128]{4,3,2,1,0:T(8,128)(2,1)} %get-tuple-element.56), channel_id=1, source_target_pairs={{0,4},{4,0},{1,5},{5,1},{2,6},{6,2},{3,7},{7,3}} | collective-permute-start | bytes 3932168 | tf_op jit(solution)/shard_map/ppermute | solution.py:511
  410.9 27.8 %collective-permute-start.1 = (bf16[16,4,10,8,128]{4,3,2,1,0:T(8,128)(2,1)}, bf16[16,4,10,8,128]{4,3,2,1,0:T(8,128)(2,1)}, u32[]{:S(2)}, u32[]{:S(2)}) collective-permute-start(bf16[16,4,10,8,128]{4,3,2,1,0:T(8,128)(2,1)} %get-tuple-element.53), channel_id=1, source_target_pairs={{0,4},{4,0},{1,5},{5,1},{2,6},{6,2},{3,7},{7,3}} | collective-permute-start | bytes 3932168 | tf_op jit(solution)/shard_map/ppermute | solution.py:511
  474.8 32.0 %collective-permute-start.21 = (bf16[32,10,16,128]{3,2,1,0:T(8,128)(2,1)}, bf16[32,10,16,128]{3,2,1,0:T(8,128)(2,1)}, u32[]{:S(2)}, u32[]{:S(2)}) collective-permute-start(bf16[32,10,16,128]{3,2,1,0:T(8,128)(2,1)} %get-tuple-element.84), channel_id=1, source_target_pairs={{0,2},{2,0},{1,3},{3,1},{4,6},{6,4},{5,7},{7,5}} | collective-permute-start | bytes 3932168 | tf_op jit(solution)/shard_map/ppermute | solution.py:508
  475.8 59.1 %collective-permute-start.6 = (bf16[32,10,16,128]{3,2,1,0:T(8,128)(2,1)}, bf16[32,10,16,128]{3,2,1,0:T(8,128)(2,1)}, u32[]{:S(2)}, u32[]{:S(2)}) collective-permute-start(bf16[32,10,16,128]{3,2,1,0:T(8,128)(2,1)} %get-tuple-element.62), channel_id=1, source_target_pairs={{0,2},{2,0},{1,3},{3,1},{4,6},{6,4},{5,7},{7,5}} | collective-permute-start | bytes 3932168 | tf_op jit(solution)/shard_map/ppermute | solution.py:508
  491.8 66.1 %collective-permute-start.11 = (bf16[32,10,16,128]{3,2,1,0:T(8,128)(2,1)}, bf16[32,10,16,128]{3,2,1,0:T(8,128)(2,1)}, u32[]{:S(2)}, u32[]{:S(2)}) collective-permute-start(bf16[32,10,16,128]{3,2,1,0:T(8,128)(2,1)} %get-tuple-element.70), channel_id=1, source_target_pairs={{0,2},{2,0},{1,3},{3,1},{4,6},{6,4},{5,7},{7,5}} | collective-permute-start | bytes 3932168 | tf_op jit(solution)/shard_map/ppermute | solution.py:508
  518.3 51.3 %collective-permute-start.22 = (bf16[16,4,10,8,128]{4,3,2,1,0:T(8,128)(2,1)}, bf16[16,4,10,8,128]{4,3,2,1,0:T(8,128)(2,1)}, u32[]{:S(2)}, u32[]{:S(2)}) collective-permute-start(bf16[16,4,10,8,128]{4,3,2,1,0:T(8,128)(2,1)} %get-tuple-element.86), channel_id=1, source_target_pairs={{0,4},{4,0},{1,5},{5,1},{2,6},{6,2},{3,7},{7,3}} | collective-permute-start | bytes 3932168 | tf_op jit(solution)/shard_map/ppermute | solution.py:511
  546.1 37.7 %collective-permute-start.7 = (bf16[16,4,10,8,128]{4,3,2,1,0:T(8,128)(2,1)}, bf16[16,4,10,8,128]{4,3,2,1,0:T(8,128)(2,1)}, u32[]{:S(2)}, u32[]{:S(2)}) collective-permute-start(bf16[16,4,10,8,128]{4,3,2,1,0:T(8,128)(2,1)} %get-tuple-element.64), channel_id=1, source_target_pairs={{0,4},{4,0},{1,5},{5,1},{2,6},{6,2},{3,7},{7,3}} | collective-permute-start | bytes 3932168 | tf_op jit(solution)/shard_map/ppermute | solution.py:511
  569.2 43.6 %collective-permute-start.12 = (bf16[16,4,10,8,128]{4,3,2,1,0:T(8,128)(2,1)}, bf16[16,4,10,8,128]{4,3,2,1,0:T(8,128)(2,1)}, u32[]{:S(2)}, u32[]{:S(2)}) collective-permute-start(bf16[16,4,10,8,128]{4,3,2,1,0:T(8,128)(2,1)} %get-tuple-element.72), channel_id=1, source_target_pairs={{0,4},{4,0},{1,5},{5,1},{2,6},{6,2},{3,7},{7,3}} | collective-permute-start | bytes 3932168 | tf_op jit(solution)/shard_map/ppermute | solution.py:511
  611.9 55.1 %collective-permute-start.25 = (bf16[32,10,16,128]{3,2,1,0:T(8,128)(2,1)}, bf16[32,10,16,128]{3,2,1,0:T(8,128)(2,1)}, u32[]{:S(2)}, u32[]{:S(2)}) collective-permute-start(bf16[32,10,16,128]{3,2,1,0:T(8,128)(2,1)} %get-tuple-element.92), channel_id=1, source_target_pairs={{0,2},{2,0},{1,3},{3,1},{4,6},{6,4},{5,7},{7,5}} | collective-permute-start | bytes 3932168 | tf_op jit(solution)/shard_map/ppermute | solution.py:508
  641.9 39.0 %collective-permute-start.23 = (bf16[32,10,16,128]{3,2,1,0:T(8,128)(2,1)}, bf16[32,10,16,128]{3,2,1,0:T(8,128)(2,1)}, u32[]{:S(2)}, u32[]{:S(2)}) collective-permute-start(bf16[32,10,16,128]{3,2,1,0:T(8,128)(2,1)} %get-tuple-element.88), channel_id=1, source_target_pairs={{0,2},{2,0},{1,3},{3,1},{4,6},{6,4},{5,7},{7,5}} | collective-permute-start | bytes 3932168 | tf_op jit(solution)/shard_map/ppermute | solution.py:508
  665.9 33.7 %collective-permute-start.19 = (bf16[32,10,16,128]{3,2,1,0:T(8,128)(2,1)}, bf16[32,10,16,128]{3,2,1,0:T(8,128)(2,1)}, u32[]{:S(2)}, u32[]{:S(2)}) collective-permute-start(bf16[32,10,16,128]{3,2,1,0:T(8,128)(2,1)} %get-tuple-element.81), channel_id=1, source_target_pairs={{0,2},{2,0},{1,3},{3,1},{4,6},{6,4},{5,7},{7,5}} | collective-permute-start | bytes 3932168 | tf_op jit(solution)/shard_map/ppermute | solution.py:508
  678.2 34.1 %collective-permute-start.26 = (bf16[16,4,10,8,128]{4,3,2,1,0:T(8,128)(2,1)}, bf16[16,4,10,8,128]{4,3,2,1,0:T(8,128)(2,1)}, u32[]{:S(2)}, u32[]{:S(2)}) collective-permute-start(bf16[16,4,10,8,128]{4,3,2,1,0:T(8,128)(2,1)} %get-tuple-element.94), channel_id=1, source_target_pairs={{0,4},{4,0},{1,5},{5,1},{2,6},{6,2},{3,7},{7,3}} | collective-permute-start | bytes 3932168 | tf_op jit(solution)/shard_map/ppermute | solution.py:511
  679.7 46.8 %collective-permute-start.17 = (bf16[32,10,16,128]{3,2,1,0:T(8,128)(2,1)}, bf16[32,10,16,128]{3,2,1,0:T(8,128)(2,1)}, u32[]{:S(2)}, u32[]{:S(2)}) collective-permute-start(bf16[32,10,16,128]{3,2,1,0:T(8,128)(2,1)} %get-tuple-element.78), channel_id=1, source_target_pairs={{0,2},{2,0},{1,3},{3,1},{4,6},{6,4},{5,7},{7,5}} | collective-permute-start | bytes 3932168 | tf_op jit(solution)/shard_map/ppermute | solution.py:508
  692.4 63.2 %collective-permute-start.24 = (bf16[16,4,10,8,128]{4,3,2,1,0:T(8,128)(2,1)}, bf16[16,4,10,8,128]{4,3,2,1,0:T(8,128)(2,1)}, u32[]{:S(2)}, u32[]{:S(2)}) collective-permute-start(bf16[16,4,10,8,128]{4,3,2,1,0:T(8,128)(2,1)} %get-tuple-element.90), channel_id=1, source_target_pairs={{0,4},{4,0},{1,5},{5,1},{2,6},{6,2},{3,7},{7,3}} | collective-permute-start | bytes 3932168 | tf_op jit(solution)/shard_map/ppermute | solution.py:511
  710.9 76.1 %collective-permute-start.20 = (bf16[16,4,10,8,128]{4,3,2,1,0:T(8,128)(2,1)}, bf16[16,4,10,8,128]{4,3,2,1,0:T(8,128)(2,1)}, u32[]{:S(2)}, u32[]{:S(2)}) collective-permute-start(bf16[16,4,10,8,128]{4,3,2,1,0:T(8,128)(2,1)} %get-tuple-element.83), channel_id=1, source_target_pairs={{0,4},{4,0},{1,5},{5,1},{2,6},{6,2},{3,7},{7,3}} | collective-permute-start | bytes 3932168 | tf_op jit(solution)/shard_map/ppermute | solution.py:511
  737.8 80.6 %collective-permute-start.18 = (bf16[16,4,10,8,128]{4,3,2,1,0:T(8,128)(2,1)}, bf16[16,4,10,8,128]{4,3,2,1,0:T(8,128)(2,1)}, u32[]{:S(2)}, u32[]{:S(2)}) collective-permute-start(bf16[16,4,10,8,128]{4,3,2,1,0:T(8,128)(2,1)} %get-tuple-element.80), channel_id=1, source_target_pairs={{0,4},{4,0},{1,5},{5,1},{2,6},{6,2},{3,7},{7,3}} | collective-permute-start | bytes 3932168 | tf_op jit(solution)/shard_map/ppermute | solution.py:511
